TPU v7x, 128 devices: a whole 4x4x4 slice. The times are simulated.
128 devices in a mesh: row: 8 (over z, core), col: 16 (over y, x).
Axes of the slice: x: 4, y: 4, z: 4, core: 2. Of those that a mesh axis runs over, the one named last changes fastest.
Arguments:
- load_amp: float32 [4096, 8192], P('row', 'col'), may hold values from 0.05 to 1
- load_mask: int32 [4096, 8192], P('row', 'col'), may hold values 0 or 1
- leak: float32 [4096, 8192], P('row', 'col'), may hold values from 0.001 to 0.05
- coarse_leak: float32 [1024, 2048], P('row', 'col'), may hold values from 0.01 to 0.5
- coarse_init: float32 [1024, 2048], P('row', 'col'), may hold values from 0 to 1
- via_fine: int32 [8, 32768], P('row', 'col'), may hold values from 0 to 262143
- via_coarse: int32 [8, 32768], P('row', 'col'), may hold values from 0 to 262143, as said below
- via_count: int32 [8, 256], P('row', 'col'), may hold values from 0 to 128, as said below
Outputs:
- fine_drop: float32 [4096, 8192], P('row', 'col')
- coarse_drop: float32 [1024, 2048], P('row', 'col')
Inputs may be any that keep to these rules, and one draw needn't show every extreme that they name: `via_coarse`: slot s of a tile names a coarse node whose stored column lies in s // 128 * 128 to s // 128 * 128 + 127. `via_count`: slots of an owner past its count are padding and carry arbitrary indices. In each tile row some owner gets 128 live slots from every tile of that row.
All inputs are finite; a program needn't handle non-finite values. No bound on the sum of `load_mask` on one device may be relied on, other than what follows from the above.
Results may differ from a plain program's by a relative error of at most 0.00022.
Values sent between devices are 32-bit elements; how exact they have to be, the bound alone decides.
A program may use at most 64 MiB of HBM per device.

v0:
```python
import functools
import jax
import jax.numpy as jnp
from jax import lax
from jax.experimental import pallas as pl
from jax.experimental.pallas import tpu as pltpu
from jax.sharding import PartitionSpec as P

GROUP = 16
ITERS = 4
LANES = 128

via_conductance = 2.0
coarse_conductance = 4.0
relaxation = 0.8

F32 = jnp.float32
BF16 = jnp.bfloat16


def divide(value, by):
    if by & (by - 1) == 0:
        return lax.shift_right_logical(value, by.bit_length() - 1)
    return value // by


def remainder(value, by):
    if by & (by - 1) == 0:
        return value & (by - 1)
    return value % by


def halves(value):
    high = value.astype(BF16).astype(F32)
    return high, value - high


def dot(a, b):
    return jnp.dot(a, b, preferred_element_type=F32)


def chunk_of(rows, top):
    size = top
    while rows % size:
        size -= 8
    return size


def kernel(
    R, C,
    amp_in, mask_in, leak_in, cleak_in, cinit_in, vf_in, vc_in, cnt_in,
    x_out, c_out,
    amp, mask, leak, cleak, cinit, vf, vc, cnt, load_sem, xv,
    msg_out, msg_in, val_out, val_in, fval_out, fval_in,
    place_v, place_s, Bt, dv, diag, V, rhs, z0, G,
    edge, E, ET, H, rtop, rbot, rcorner,
    seen, red_out, red_in, red2_out, red2_in,
    volt1, turn, seam_out, crow_top, crow_bot, cleft, cright,
    send_sem, recv_sem,
):
    row, col = lax.axis_index("row"), lax.axis_index("col")
    sources_of = (cnt_in, vc_in, vf_in, cinit_in, leak_in, cleak_in, amp_in, mask_in)
    targets_of = (cnt, vc, vf, cinit, leak, cleak, amp, mask)
    loads = [
        pltpu.make_async_copy(source, target, load_sem.at[n])
        for n, (source, target) in enumerate(zip(sources_of, targets_of))
    ]
    for load in loads:
        load.start()
    TR, TC = leak.shape
    BR, BC = cleak.shape
    S = vf.shape[1]
    per = S // C
    up, down = lax.rem(row + R - 1, R), lax.rem(row + 1, R)
    left, right = lax.rem(col + C - 1, C), lax.rem(col + 1, C)

    barrier = pltpu.get_barrier_semaphore()
    peers = [(row, lax.rem(col + d, C)) for d in range(1, C)]
    peers += [(lax.rem(row + d, R), col) for d in range(1, R)]
    peers += [(u, s) for u in (up, down) for s in (left, right)]
    for peer in peers:
        pl.semaphore_signal(barrier, inc=1, device_id=peer, device_id_type=pl.DeviceIdType.MESH)

    count = [0]
    pending = []

    def send(src, dst, device):
        n = count[0]
        count[0] += 1
        copy = pltpu.make_async_remote_copy(
            src_ref=src, dst_ref=dst, send_sem=send_sem.at[n], recv_sem=recv_sem.at[n],
            device_id=device, device_id_type=pl.DeviceIdType.MESH,
        )
        copy.start()
        pending.append(copy)
        return copy

    loads[0].wait()
    loads[1].wait()
    lane = lax.broadcasted_iota(jnp.int32, (1, per), 1)
    for o in range(C):
        msg_out[o] = jnp.where(lane < cnt[0, o], vc[:, o * per : (o + 1) * per], -1)
    msg_in[col] = msg_out[col]

    pl.semaphore_wait(barrier, len(peers))

    messages = [
        send(msg_out.at[lax.rem(col + d, C)], msg_in.at[col], (row, lax.rem(col + d, C)))
        for d in range(1, C)
    ]

    def coarse_send(ref, n):
        return [
            send(ref.at[pl.ds(0, 8)], crow_bot.at[n], (up, col)),
            send(ref.at[pl.ds(BR - 8, 8)], crow_top.at[n], (down, col)),
            send(seam_out.at[n, 0], cright.at[n], (row, left)),
            send(seam_out.at[n, 1], cleft.at[n], (row, right)),
        ]

    groups = BC // GROUP

    def seams(volt, n):
        turn[n] = volt.T
        seam_out[n, 0] = turn[n, pl.ds(0, groups, stride=GROUP), :]
        seam_out[n, 1] = turn[n, pl.ds(GROUP - 1, groups, stride=GROUP), :]

    loads[2].wait()
    weight = jnp.concatenate(
        [jnp.where(lane < cnt[0, o], via_conductance, 0.0).astype(F32) for o in range(C)], axis=1
    )
    fine = vf[...]
    fine_row = divide(fine, TC)
    fine_col = remainder(fine, TC)
    TE = TR + 32
    blocks = TC // LANES
    all_blocks = blocks + 1
    place_v[...] = divide(fine_col, LANES) * TE + (fine_row + 16)
    move = pltpu.make_async_copy(place_v, place_s, load_sem.at[9])
    move.start()
    lanes = lax.broadcasted_iota(jnp.int32, (per, TC), 1).astype(F32)
    for o in range(C):
        cut = slice(o * per, (o + 1) * per)
        turned = jnp.broadcast_to(fine_col[:, cut].astype(F32), (LANES, per)).T
        wide = jnp.concatenate([turned] * blocks, axis=1)
        Bt[cut, :] = jnp.where(wide == lanes, 1.0, 0.0).astype(BF16)

    loads[3].wait()
    seams(cinit[...], 0)
    coarse0 = coarse_send(cinit, 0)

    def ext(k, b, start, size):
        return pl.ds((k * all_blocks + b) * TE + start, size)

    def own(b, start, size):
        return pl.ds(b * TR + start, size)

    def part(b):
        return slice(b * LANES, (b + 1) * LANES)

    zero_pad = jnp.zeros((8, LANES), F32)
    for n in range(ITERS):
        for b in range(all_blocks):
            V[ext(n, b, 0, 8), :] = zero_pad
            V[ext(n, b, TR + 24, 8), :] = zero_pad

    loads[4].wait()
    wide_step = 256 if TR % 256 == 0 else 64
    half_step = wide_step // 2

    def diagonal(i, carry):
        base = pl.multiple_of(i * wide_step, wide_step)
        place = lax.broadcasted_iota(jnp.int32, (wide_step, S), 0) + i * wide_step
        match = place == fine_row
        added = dot(jnp.where(match, weight, 0.0).astype(BF16), Bt[...])
        for b in range(blocks):
            value = 4.0 + leak[pl.ds(base, wide_step), part(b)] + added[:, part(b)]
            diag[own(b, base, wide_step), :] = value
            dv[ext(0, b, base + 16, wide_step), :] = 1.0 / value
        return carry

    lax.fori_loop(0, TR // wide_step, diagonal, 0)

    low_side = lax.broadcasted_iota(jnp.int32, (TR, LANES), 1) < LANES // 2

    def halo_send(F, n):
        sides = jnp.where(
            low_side, F[ext(0, 0, 16, TR), :], F[ext(0, blocks - 1, 16, TR), :]
        )
        E[n, 0] = sides[0:8]
        E[n, 1] = sides[TR - 8 : TR]
        turned = sides.T
        ET[n, 0] = turned[0:8]
        ET[n, 1] = turned[LANES - 8 : LANES]
        for b in range(blocks):
            edge[n, 0, b] = F[ext(0, b, 16, 8), :]
            edge[n, 1, b] = F[ext(0, b, TR + 8, 8), :]
        return [
            send(E.at[n, 0], rcorner.at[n, 3], (up, left)),
            send(E.at[n, 0], rcorner.at[n, 2], (up, right)),
            send(E.at[n, 1], rcorner.at[n, 1], (down, left)),
            send(E.at[n, 1], rcorner.at[n, 0], (down, right)),
            send(ET.at[n, 0], H.at[n, 0], (row, left)),
            send(ET.at[n, 1], H.at[n, 1], (row, right)),
            send(edge.at[n, 0], rbot.at[n], (up, col)),
            send(edge.at[n, 1], rtop.at[n], (down, col)),
        ]

    top_ok, bot_ok = row > 0, row < R - 1
    left_ok, right_ok = col > 0, col < C - 1

    def keep(ok, value):
        return value * jnp.where(ok, 1.0, 0.0).astype(F32)

    def halo_land(F, n, copies):
        for copy in copies:
            copy.wait_recv()
        for b in range(blocks):
            F[ext(0, b, 8, 8), :] = keep(top_ok, rtop[n, b])
            F[ext(0, b, TR + 16, 8), :] = keep(bot_ok, rbot[n, b])
        low, high = keep(right_ok, H[n, 0]), keep(left_ok, H[n, 1])
        side = jnp.concatenate([low, jnp.zeros((LANES - 16, TR), F32), high], axis=0)
        F[ext(0, blocks, 16, TR), :] = side.T
        low8 = lax.broadcasted_iota(jnp.int32, (8, LANES), 1)
        near_low, near_high = low8 < 8, low8 >= LANES - 8

        def corner(ok, lo, hi):
            return keep(
                ok,
                jnp.where(near_low, keep(right_ok, lo), 0.0)
                + jnp.where(near_high, keep(left_ok, hi), 0.0),
            )

        F[ext(0, blocks, 8, 8), :] = corner(top_ok, rcorner[n, 1], rcorner[n, 0])
        F[ext(0, blocks, TR + 16, 8), :] = corner(bot_ok, rcorner[n, 3], rcorner[n, 2])

    for copy in messages:
        copy.wait_recv()
    heard = jnp.concatenate([msg_in[t] for t in range(C)], axis=1)
    in_row = divide(heard, BC * C)
    in_col = remainder(heard, BC)
    place_r = lax.broadcasted_iota(jnp.int32, (BR, S), 0)
    place_c = lax.broadcasted_iota(jnp.int32, (BC, S), 0)
    row_hit = place_r == in_row
    col_hot = jnp.where(place_c == in_col, 1.0, 0.0).astype(BF16)
    hi, lo = halves(cinit[...])
    glimpse = dot(hi.astype(BF16), col_hot) + dot(lo.astype(BF16), col_hot)
    at_via = jnp.sum(jnp.where(row_hit, glimpse, 0.0), axis=0, keepdims=True)
    for t in range(C):
        val_out[t] = at_via[:, t * per : (t + 1) * per]
    val_in[col] = val_out[col]
    values = [
        send(val_out.at[lax.rem(col + d, C)], val_in.at[col], (row, lax.rem(col + d, C)))
        for d in range(1, C)
    ]

    dinv_copies = halo_send(dv, 0)

    def onto_coarse(amount):
        spread = jnp.where(row_hit, amount, 0.0).astype(BF16)
        return lax.dot_general(spread, col_hot, (((1,), (1,)), ((), ())), preferred_element_type=F32)

    loads[5].wait()
    coarse_diag = 4.0 * coarse_conductance + cleak[...] + onto_coarse(via_conductance)

    for copy in values:
        copy.wait_recv()
    loads[6].wait()
    loads[7].wait()
    drops = weight * jnp.concatenate([val_in[o] for o in range(C)], axis=1)
    drop_hi, drop_lo = halves(drops)

    def inject(i, carry):
        base = pl.multiple_of(i * half_step, half_step)
        place = lax.broadcasted_iota(jnp.int32, (half_step, S), 0) + i * half_step
        match = place == fine_row
        both = [jnp.where(match, part_of, 0.0).astype(BF16) for part_of in (drop_hi, drop_lo)]
        both = dot(jnp.concatenate(both, axis=0), Bt[...])
        added = both[:half_step] + both[half_step:]
        at = pl.ds(base, half_step)
        for b in range(blocks):
            value = amp[at, part(b)] * mask[at, part(b)].astype(F32) + added[:, part(b)]
            rhs[own(b, base, half_step), :] = value
            V[ext(0, b, base + 16, half_step), :] = value * dv[ext(0, b, base + 16, half_step), :]
        return carry

    lax.fori_loop(0, TR // half_step, inject, 0)
    first_copies = halo_send(V, 1)
    halo_land(dv, 0, dinv_copies)
    halo_land(V, 1, first_copies)

    rows = chunk_of(TR + 16, 48)

    def around(k, start, size, count):
        first = lax.broadcasted_iota(jnp.int32, (size, LANES), 1) == 0
        last = lax.broadcasted_iota(jnp.int32, (size, LANES), 1) == LANES - 1
        mid = [V[ext(k, b, start, size), :] for b in range(all_blocks)]
        after = [pltpu.roll(m, LANES - 1, 1) for m in mid]
        before = [pltpu.roll(m, 1, 1) for m in mid]
        found = []
        for b in range(count):
            tall = V[ext(k, b, start - 1, size), :] + V[ext(k, b, start + 1, size), :]
            left_of = jnp.where(first, before[b - 1], before[b])
            right_of = jnp.where(last, after[(b + 1) % all_blocks], after[b])
            found.append(tall + (left_of + right_of))
        return mid, found

    for k in range(ITERS - 1):

        def advance(i, carry, k=k):
            start = pl.multiple_of(8 + i * rows, 8)
            near = around(k, start, rows, all_blocks)[1]
            for b in range(all_blocks):
                fresh = dv[ext(0, b, start, rows), :] * near[b]
                if k:
                    fresh = (fresh + fresh) - V[ext(k - 1, b, start, rows), :]
                V[ext(k + 1, b, start, rows), :] = fresh
            return carry

        lax.fori_loop(0, (TR + 16) // rows, advance, 0)

    orders = 2 * ITERS - 1
    sums = orders + ITERS
    tall_step = 32

    def residue(i, carry):
        base = pl.multiple_of(i * tall_step, tall_step)
        near = around(0, base + 16, tall_step, blocks)[1]
        for b in range(blocks):
            z0[own(b, base, tall_step), :] = rhs[own(b, base, tall_step), :] - near[b]
        return carry

    lax.fori_loop(0, TR // tall_step, residue, 0)

    def fold(value):
        total = value[0:8]
        for n in range(1, tall_step // 8):
            total = total + value[n * 8 : n * 8 + 8]
        return total

    def gram(i, carry):
        base = pl.multiple_of(i * tall_step, tall_step)
        mid, near = around(ITERS - 1, base + 16, tall_step, blocks)
        totals = list(carry)
        for b in range(blocks):
            at = own(b, base, tall_step)
            v = [V[ext(k, b, base + 16, tall_step), :] for k in range(ITERS - 1)] + [mid[b]]
            source, low, high = rhs[at, :], z0[at, :], diag[at, :] * mid[b] - near[b]
            fresh = [fold(low * v[k]) for k in range(ITERS)]
            fresh += [fold(high * v[k]) for k in range(1, ITERS)]
            fresh += [fold(source * v[k]) for k in range(ITERS)]
            totals = [x + y for x, y in zip(totals, fresh)]
        return tuple(totals)

    totals = lax.fori_loop(
        0, TR // tall_step, gram, tuple(jnp.zeros((8, LANES), F32) for _ in range(sums))
    )
    flat = jnp.concatenate(
        [jnp.sum(total, axis=0, keepdims=True) for total in totals]
        + [jnp.zeros((16 - sums, LANES), F32)], axis=0,
    )
    same = lax.broadcasted_iota(jnp.int32, (16, LANES), 0) == lax.broadcasted_iota(
        jnp.int32, (16, LANES), 1
    )
    number = jnp.sum(flat, axis=1, keepdims=True)
    red_out[...] = jnp.sum(jnp.where(same, number, 0.0), axis=0, keepdims=True)
    copies = [
        send(red_out, red_in.at[d - 1], (row, lax.rem(col + d, C))) for d in range(1, C)
    ]

    move.wait()
    reach = 32

    def fetch(i, carry):
        for j in range(reach):
            s = i * reach + j
            at = place_s[0, s]
            for k in range(ITERS):
                G[pl.ds(k * S + s, 1), :] = V[pl.ds(k * all_blocks * TE + at, 1), :]
        return carry

    lax.fori_loop(0, S // reach, fetch, 0)
    total = red_out[...]
    for d, copy in enumerate(copies):
        copy.wait_recv()
        total = total + red_in[d]
    red2_out[...] = total
    copies = [
        send(red2_out, red2_in.at[d - 1], (lax.rem(row + d, R), col)) for d in range(1, R)
    ]
    turned_lane = lax.broadcasted_iota(jnp.int32, (LANES, per), 0)
    fine_lane = remainder(fine_col, LANES)
    seen_at = [[] for _ in range(ITERS)]
    for o in range(C):
        pick = turned_lane == fine_lane[:, o * per : (o + 1) * per]
        for k in range(ITERS):
            turned = G[pl.ds(k * S + o * per, per), :].T
            seen_at[k].append(jnp.sum(jnp.where(pick, turned, 0.0), axis=0, keepdims=True))
    for k in range(ITERS):
        seen[k] = jnp.concatenate(seen_at[k], axis=1)
    for d, copy in enumerate(copies):
        copy.wait_recv()
        total = total + red2_in[d]
    number = jnp.sum(jnp.where(same, jnp.broadcast_to(total, (16, LANES)), 0.0), axis=1, keepdims=True)
    number = [number[n : n + 1, :] for n in range(sums)]

    matrix = [[None] * (ITERS + 1) for _ in range(ITERS)]
    for n in range(ITERS, orders):
        number[n] = 2.0 * number[n] - number[2 * (ITERS - 1) - n]
    for j in range(ITERS):
        for k in range(j + 1):
            matrix[j][k] = matrix[k][j] = 0.5 * (number[j + k] + number[j - k])
        matrix[j][ITERS] = number[orders + j]
    for i in range(ITERS):
        inverse = 1.0 / matrix[i][i]
        for k in range(i + 1, ITERS + 1):
            matrix[i][k] = matrix[i][k] * inverse
        for j in range(i + 1, ITERS):
            for k in range(i + 1, ITERS + 1):
                matrix[j][k] = matrix[j][k] - matrix[j][i] * matrix[i][k]
    coef = [None] * ITERS
    for i in reversed(range(ITERS)):
        coef[i] = matrix[i][ITERS]
        for k in range(i + 1, ITERS):
            coef[i] = coef[i] - matrix[i][k] * coef[k]

    at_fine = coef[0] * seen[0]
    for k in range(1, ITERS):
        at_fine = at_fine + coef[k] * seen[k]
    store = pltpu.make_async_copy(xv, x_out, load_sem.at[8])
    for o in range(C):
        fval_out[o] = at_fine[:, o * per : (o + 1) * per]
    fval_in[col] = fval_out[col]
    copies = [
        send(fval_out.at[lax.rem(col + d, C)], fval_in.at[col], (row, lax.rem(col + d, C)))
        for d in range(1, C)
    ]


    def finish(i, carry):
        base = pl.multiple_of(i * step, step)
        for b in range(blocks):
            value = coef[0] * V[ext(0, b, base + 16, step), :]
            for k in range(1, ITERS):
                value = value + coef[k] * V[ext(k, b, base + 16, step), :]
            xv[pl.ds(base, step), part(b)] = value
        return carry

    step = 64
    lax.fori_loop(0, TR // step, finish, 0)
    store.start()
    place = lax.broadcasted_iota(jnp.int32, (BR, BC), 1)
    place_u = lax.broadcasted_iota(jnp.int32, (BR, BC), 0)
    within = remainder(place, GROUP)

    def beside(volt, n):
        above = jnp.where(place_u == 0, keep(top_ok, crow_top[n, 7:8, :]), pltpu.roll(volt, 1, 0))
        below = jnp.where(
            place_u == BR - 1, keep(bot_ok, crow_bot[n, 0:1, :]), pltpu.roll(volt, BR - 1, 0)
        )
        group = lax.broadcasted_iota(jnp.int32, (groups, BR), 0)
        far = cleft[n]
        turn[n, pl.ds(0, groups, stride=GROUP), :] = jnp.where(
            left_ok, far, jnp.where(group == 0, 0.0, jnp.roll(far, 1, 0))
        )
        far = cright[n]
        turn[n, pl.ds(GROUP - 1, groups, stride=GROUP), :] = jnp.where(
            right_ok, far, jnp.where(group == groups - 1, 0.0, jnp.roll(far, -1, 0))
        )
        edge = turn[n].T
        before = jnp.where(within == 0, edge, pltpu.roll(volt, 1, 1))
        after = jnp.where(within == GROUP - 1, edge, pltpu.roll(volt, BC - 1, 1))
        return above + below + before + after

    for copy in coarse0:
        copy.wait_recv()
    volt = cinit[...]
    scale = relaxation / coarse_diag
    partial = volt + scale * (coarse_conductance * beside(volt, 0) - coarse_diag * volt)
    for copy in copies:
        copy.wait_recv()
    amount = via_conductance * jnp.concatenate([fval_in[t] for t in range(C)], axis=1)
    hi, lo = halves(amount)
    sources = onto_coarse(hi) + onto_coarse(lo)
    volt = partial + scale * sources
    volt1[...] = volt
    seams(volt, 1)
    coarse1 = coarse_send(volt1, 1)
    partial = volt + scale * (sources - coarse_diag * volt)
    for copy in coarse1:
        copy.wait_recv()
    c_out[...] = partial + scale * (coarse_conductance * beside(volt, 1))
    store.wait()
    for copy in pending:
        copy.wait_send()


def per_device(R, C, load_amp, load_mask, leak, coarse_leak, coarse_init, via_fine, via_coarse, via_count):
    TR, TC = leak.shape
    BR, BC = coarse_leak.shape
    S = via_fine.shape[1]
    per = S // C
    copies = 4 * (C - 1) + (R - 1) + 24
    vmem = pl.BlockSpec(memory_space=pltpu.VMEM)
    blocks = TC // LANES
    ext = (blocks + 1) * (TR + 32)
    return pl.pallas_call(
        functools.partial(kernel, R, C),
        out_shape=(jax.ShapeDtypeStruct((TR, TC), F32), jax.ShapeDtypeStruct((BR, BC), F32)),
        in_specs=[pl.BlockSpec(memory_space=pltpu.HBM)] * 8,
        out_specs=(pl.BlockSpec(memory_space=pltpu.HBM), vmem),
        scratch_shapes=[
            pltpu.VMEM((TR, TC), F32), pltpu.VMEM((TR, TC), jnp.int32), pltpu.VMEM((TR, TC), F32),
            pltpu.VMEM((BR, BC), F32), pltpu.VMEM((BR, BC), F32),
            pltpu.VMEM((1, S), jnp.int32), pltpu.VMEM((1, S), jnp.int32),
            pltpu.SMEM((1, C), jnp.int32), pltpu.SemaphoreType.DMA((10,)), pltpu.VMEM((TR, TC), F32),
            pltpu.VMEM((C, 1, per), jnp.int32), pltpu.VMEM((C, 1, per), jnp.int32),
            pltpu.VMEM((C, 1, per), F32), pltpu.VMEM((C, 1, per), F32),
            pltpu.VMEM((C, 1, per), F32), pltpu.VMEM((C, 1, per), F32),
            pltpu.VMEM((1, S), jnp.int32), pltpu.SMEM((1, S), jnp.int32),
            pltpu.VMEM((S, TC), BF16),
            pltpu.VMEM((ext, LANES), F32),
            pltpu.VMEM((blocks * TR, LANES), F32),
            pltpu.VMEM((ITERS * ext, LANES), F32),
            pltpu.VMEM((blocks * TR, LANES), F32),
            pltpu.VMEM((blocks * TR, LANES), F32),
            pltpu.VMEM((ITERS * S, LANES), F32),
            pltpu.VMEM((2, 2, blocks, 8, LANES), F32),
            pltpu.VMEM((2, 2, 8, LANES), F32),
            pltpu.VMEM((2, 2, 8, TR), F32),
            pltpu.VMEM((2, 2, 8, TR), F32),
            pltpu.VMEM((2, blocks, 8, LANES), F32),
            pltpu.VMEM((2, blocks, 8, LANES), F32),
            pltpu.VMEM((2, 4, 8, LANES), F32),
            pltpu.VMEM((ITERS, 1, S), F32),
            pltpu.VMEM((1, LANES), F32), pltpu.VMEM((C - 1, 1, LANES), F32),
            pltpu.VMEM((1, LANES), F32), pltpu.VMEM((R - 1, 1, LANES), F32),
            pltpu.VMEM((BR, BC), F32),
            pltpu.VMEM((2, BC, BR), F32), pltpu.VMEM((2, 2, BC // GROUP, BR), F32),
            pltpu.VMEM((2, 8, BC), F32), pltpu.VMEM((2, 8, BC), F32),
            pltpu.VMEM((2, BC // GROUP, BR), F32), pltpu.VMEM((2, BC // GROUP, BR), F32),
            pltpu.SemaphoreType.DMA((copies,)),
            pltpu.SemaphoreType.DMA((copies,)),
        ],
        compiler_params=pltpu.CompilerParams(
            collective_id=0, has_side_effects=True, vmem_limit_bytes=60 * 1024 * 1024
        ),
    )(load_amp, load_mask, leak, coarse_leak, coarse_init, via_fine, via_coarse, via_count)


def solution(mesh):
    spec = P("row", "col")
    return jax.shard_map(
        functools.partial(per_device, mesh.shape["row"], mesh.shape["col"]),
        mesh=mesh, in_specs=(spec,) * 8, out_specs=(spec, spec), check_vma=False,
    )
```

profile of v0, /device:TPU:0, one launch (start us, length us, event | category | flops | bytes accessed | tf_op | source)
XLA Modules:
  0.0 57.7 jit_solution(14043550373495021632)
XLA Ops:
  0.6 54.1 %shard_map.95 = (f32[512,512]{1,0:T(8,128)}, f32[128,128]{1,0:T(8,128)}) custom-call(f32[512,512]{1,0:T(8,128)} %amp_in.1, s32[512,512]{1,0:T(8,128)} %mask_in.1, f32[512,512]{1,0:T(8,128)} %leak_in.1, f32[128,128]{1,0:T(8,128)} %cleak_in.1, f32[128,128]{1,0:T(8,128)} %cinit_in.1, s32[1,2048]{1,0:T(1,128)} %vf_in.1, s32[1,2048]{1,0:T(1,128)} %vc_in.1, ...), custom_call_target="tpu_custom_call" | custom-call | tf_op jit(solution)/shard_map/pallas_call | solution.py:506
  54.7 0.0 copy-start
  54.7 2.3 %copy.12 = f32[512,512]{1,0:T(8,128)} copy(f32[512,512]{1,0:T(8,128)} %get-tuple-element.4) | data formatting | bytes 2097152
  57.0 0.0 copy-done
  57.0 0.6 %copy.13 = f32[128,128]{1,0:T(8,128)} copy(f32[128,128]{1,0:T(8,128)S(1)} %copy-done) | data formatting | bytes 131072
Async XLA Ops:
  54.7 2.3 %copy-start = (f32[128,128]{1,0:T(8,128)S(1)}, f32[128,128]{1,0:T(8,128)}, u32[]{:S(2)}) copy-start(f32[128,128]{1,0:T(8,128)} %get-tuple-element.5) | copy-start | bytes 196612
where the time goes:
time: 57.8 us; the launch traced here: 57.7 us
  Pallas kernels  54.1 us (94%)
  local copies, waits for them, and re-layouts  2.93 us (5%)
  between operations  0.65 us (1%)
    pallas_call x1, Pallas kernels, per_device(): pl.pallas_call(functools.partial(kernel, R, C), out_shape=(jax.ShapeDtype...  54.1 us
    unnamed x4, local copies, waits for them, and re-layouts  2.93 us

commit v1 on v0

--- a/solution.py
+++ b/solution.py
@@ -50,9 +50,9 @@
     R, C,
     amp_in, mask_in, leak_in, cleak_in, cinit_in, vf_in, vc_in, cnt_in,
     x_out, c_out,
-    amp, mask, leak, cleak, cinit, vf, vc, cnt, load_sem, xv,
+    amp, mask, leak, cleak, cinit, vf, vc, cnt, load_sem,
     msg_out, msg_in, val_out, val_in, fval_out, fval_in,
-    place_v, place_s, Bt, dv, diag, V, rhs, z0, G,
+    place_v, place_s, Bt, dv, diag, V, rhs, W, G,
     edge, E, ET, H, rtop, rbot, rcorner,
     seen, red_out, red_in, red2_out, red2_in,
     volt1, turn, seam_out, crow_top, crow_bot, cleft, cright,
@@ -134,8 +134,8 @@
     TE = TR + 32
     blocks = TC // LANES
     all_blocks = blocks + 1
-    place_v[...] = divide(fine_col, LANES) * TE + (fine_row + 16)
-    move = pltpu.make_async_copy(place_v, place_s, load_sem.at[9])
+    place_v[...] = (divide(fine_col, LANES) * TR + fine_row) * ITERS
+    move = pltpu.make_async_copy(place_v, place_s, load_sem.at[8])
     move.start()
     lanes = lax.broadcasted_iota(jnp.int32, (per, TC), 1).astype(F32)
     for o in range(C):
@@ -288,7 +288,7 @@
     halo_land(dv, 0, dinv_copies)
     halo_land(V, 1, first_copies)
 
-    rows = chunk_of(TR + 16, 48)
+    rows = chunk_of(TR + 16, 176)
 
     def around(k, start, size, count):
         first = lax.broadcasted_iota(jnp.int32, (size, LANES), 1) == 0
@@ -320,16 +320,7 @@
 
     orders = 2 * ITERS - 1
     sums = orders + ITERS
-    tall_step = 32
-
-    def residue(i, carry):
-        base = pl.multiple_of(i * tall_step, tall_step)
-        near = around(0, base + 16, tall_step, blocks)[1]
-        for b in range(blocks):
-            z0[own(b, base, tall_step), :] = rhs[own(b, base, tall_step), :] - near[b]
-        return carry
-
-    lax.fori_loop(0, TR // tall_step, residue, 0)
+    tall_step = 64
 
     def fold(value):
         total = value[0:8]
@@ -344,7 +335,10 @@
         for b in range(blocks):
             at = own(b, base, tall_step)
             v = [V[ext(k, b, base + 16, tall_step), :] for k in range(ITERS - 1)] + [mid[b]]
-            source, low, high = rhs[at, :], z0[at, :], diag[at, :] * mid[b] - near[b]
+            source, held = rhs[at, :], diag[at, :]
+            low, high = held * (v[0] - v[1]), held * mid[b] - near[b]
+            for k in range(ITERS):
+                W[pl.ds((b * TR + base) * ITERS + k, tall_step, stride=ITERS), :] = v[k]
             fresh = [fold(low * v[k]) for k in range(ITERS)]
             fresh += [fold(high * v[k]) for k in range(1, ITERS)]
             fresh += [fold(source * v[k]) for k in range(ITERS)]
@@ -373,30 +367,28 @@
     def fetch(i, carry):
         for j in range(reach):
             s = i * reach + j
-            at = place_s[0, s]
-            for k in range(ITERS):
-                G[pl.ds(k * S + s, 1), :] = V[pl.ds(k * all_blocks * TE + at, 1), :]
+            G[pl.ds(s * ITERS, ITERS), :] = W[pl.ds(place_s[0, s], ITERS), :]
         return carry
 
     lax.fori_loop(0, S // reach, fetch, 0)
-    total = red_out[...]
-    for d, copy in enumerate(copies):
-        copy.wait_recv()
-        total = total + red_in[d]
-    red2_out[...] = total
-    copies = [
-        send(red2_out, red2_in.at[d - 1], (lax.rem(row + d, R), col)) for d in range(1, R)
-    ]
     turned_lane = lax.broadcasted_iota(jnp.int32, (LANES, per), 0)
     fine_lane = remainder(fine_col, LANES)
     seen_at = [[] for _ in range(ITERS)]
     for o in range(C):
         pick = turned_lane == fine_lane[:, o * per : (o + 1) * per]
         for k in range(ITERS):
-            turned = G[pl.ds(k * S + o * per, per), :].T
+            turned = G[pl.ds(o * per * ITERS + k, per, stride=ITERS), :].T
             seen_at[k].append(jnp.sum(jnp.where(pick, turned, 0.0), axis=0, keepdims=True))
     for k in range(ITERS):
         seen[k] = jnp.concatenate(seen_at[k], axis=1)
+    total = red_out[...]
+    for d, copy in enumerate(copies):
+        copy.wait_recv()
+        total = total + red_in[d]
+    red2_out[...] = total
+    copies = [
+        send(red2_out, red2_in.at[d - 1], (lax.rem(row + d, R), col)) for d in range(1, R)
+    ]
     for d, copy in enumerate(copies):
         copy.wait_recv()
         total = total + red2_in[d]
@@ -426,7 +418,6 @@
     at_fine = coef[0] * seen[0]
     for k in range(1, ITERS):
         at_fine = at_fine + coef[k] * seen[k]
-    store = pltpu.make_async_copy(xv, x_out, load_sem.at[8])
     for o in range(C):
         fval_out[o] = at_fine[:, o * per : (o + 1) * per]
     fval_in[col] = fval_out[col]
@@ -442,12 +433,11 @@
             value = coef[0] * V[ext(0, b, base + 16, step), :]
             for k in range(1, ITERS):
                 value = value + coef[k] * V[ext(k, b, base + 16, step), :]
-            xv[pl.ds(base, step), part(b)] = value
+            x_out[pl.ds(base, step), part(b)] = value
         return carry
 
     step = 64
     lax.fori_loop(0, TR // step, finish, 0)
-    store.start()
     place = lax.broadcasted_iota(jnp.int32, (BR, BC), 1)
     place_u = lax.broadcasted_iota(jnp.int32, (BR, BC), 0)
     within = remainder(place, GROUP)
@@ -489,7 +479,6 @@
     for copy in coarse1:
         copy.wait_recv()
     c_out[...] = partial + scale * (coarse_conductance * beside(volt, 1))
-    store.wait()
     for copy in pending:
         copy.wait_send()
 
@@ -505,14 +494,14 @@
     ext = (blocks + 1) * (TR + 32)
     return pl.pallas_call(
         functools.partial(kernel, R, C),
-        out_shape=(jax.ShapeDtypeStruct((TR, TC), F32), jax.ShapeDtypeStruct((BR, BC), F32)),
+        out_shape=(pltpu.VMEM((TR, TC), F32), pltpu.VMEM((BR, BC), F32)),
         in_specs=[pl.BlockSpec(memory_space=pltpu.HBM)] * 8,
-        out_specs=(pl.BlockSpec(memory_space=pltpu.HBM), vmem),
+        out_specs=(vmem, vmem),
         scratch_shapes=[
             pltpu.VMEM((TR, TC), F32), pltpu.VMEM((TR, TC), jnp.int32), pltpu.VMEM((TR, TC), F32),
             pltpu.VMEM((BR, BC), F32), pltpu.VMEM((BR, BC), F32),
             pltpu.VMEM((1, S), jnp.int32), pltpu.VMEM((1, S), jnp.int32),
-            pltpu.SMEM((1, C), jnp.int32), pltpu.SemaphoreType.DMA((10,)), pltpu.VMEM((TR, TC), F32),
+            pltpu.SMEM((1, C), jnp.int32), pltpu.SemaphoreType.DMA((9,)),
             pltpu.VMEM((C, 1, per), jnp.int32), pltpu.VMEM((C, 1, per), jnp.int32),
             pltpu.VMEM((C, 1, per), F32), pltpu.VMEM((C, 1, per), F32),
             pltpu.VMEM((C, 1, per), F32), pltpu.VMEM((C, 1, per), F32),
@@ -522,7 +511,7 @@
             pltpu.VMEM((blocks * TR, LANES), F32),
             pltpu.VMEM((ITERS * ext, LANES), F32),
             pltpu.VMEM((blocks * TR, LANES), F32),
-            pltpu.VMEM((blocks * TR, LANES), F32),
+            pltpu.VMEM((ITERS * blocks * TR, LANES), F32),
             pltpu.VMEM((ITERS * S, LANES), F32),
             pltpu.VMEM((2, 2, blocks, 8, LANES), F32),
             pltpu.VMEM((2, 2, 8, LANES), F32),

time: 57.8 us -> 52.6 us (0.910)
  Pallas kernels: 54.1 us -> 50.3 us
  local copies, waits for them, and re-layouts: 2.93 us -> 1.6 us
    pallas_call x1, Pallas kernels: 54.1 us -> 50.3 us  [per_device(): pl.pallas_call(functools.partial(kernel, R, C), out_shape=(pltpu.VMEM((TR...]
    unnamed x4 -> x2, local copies, waits for them, and re-layouts: 2.93 us -> 1.6 us
where the time goes in v1:
time: 52.6 us; the launch traced here: 52.5 us
  Pallas kernels  50.3 us (96%)
  local copies, waits for them, and re-layouts  1.6 us (3%)
  between operations  0.64 us (1%)
    pallas_call x1, Pallas kernels, per_device(): pl.pallas_call(functools.partial(kernel, R, C), out_shape=(pltpu.VMEM((TR...  50.3 us
    unnamed x2, local copies, waits for them, and re-layouts  1.6 us

profile of v1, /device:TPU:0, one launch (start us, length us, event | category | flops | bytes accessed | tf_op | source)
XLA Modules:
  0.0 52.5 jit_solution(17949972923227993597)
XLA Ops:
  0.6 50.3 %shard_map.95 = (f32[512,512]{1,0:T(8,128)S(1)}, f32[128,128]{1,0:T(8,128)S(1)}) custom-call(f32[512,512]{1,0:T(8,128)} %amp_in.1, s32[512,512]{1,0:T(8,128)} %mask_in.1, f32[512,512]{1,0:T(8,128)} %leak_in.1, f32[128,128]{1,0:T(8,128)} %cleak_in.1, f32[128,128]{1,0:T(8,128)} %cinit_in.1, s32[1,2048]{1,0:T(1,128)} %vf_in.1, s32[1,2048]{1,0:T(1,128)} %vc_in.1, ...), custom_call_target="tpu_custom_call" | custom-call | tf_op jit(solution)/shard_map/pallas_call | solution.py:495
  50.9 1.0 %copy.12 = f32[512,512]{1,0:T(8,128)} copy(f32[512,512]{1,0:T(8,128)S(1)} %get-tuple-element.2) | data formatting | bytes 2097152
  51.9 0.6 %copy.13 = f32[128,128]{1,0:T(8,128)} copy(f32[128,128]{1,0:T(8,128)S(1)} %get-tuple-element.3) | data formatting | bytes 131072

commit v2 on v1

v2 whole, which is shorter than its diff:
```python
import functools
import jax
import jax.numpy as jnp
from jax import lax
from jax.experimental import pallas as pl
from jax.experimental.pallas import tpu as pltpu
from jax.sharding import PartitionSpec as P

GROUP = 16
ITERS = 4
LANES = 128

via_conductance = 2.0
coarse_conductance = 4.0
relaxation = 0.8

F32 = jnp.float32
BF16 = jnp.bfloat16


def divide(value, by):
    if by & (by - 1) == 0:
        return lax.shift_right_logical(value, by.bit_length() - 1)
    return value // by


def remainder(value, by):
    if by & (by - 1) == 0:
        return value & (by - 1)
    return value % by


def halves(value):
    high = value.astype(BF16).astype(F32)
    return high, value - high


def dot(a, b):
    return jnp.dot(a, b, preferred_element_type=F32)


def chunk_of(rows, top):
    size = top
    while rows % size:
        size -= 8
    return size


def ring_order(C):
    side = 4 if C % 4 == 0 else C
    tall = C // side

    def reach(d, n):
        return min(d, n - d)

    offsets = sorted(
        ((dy, dx) for dy in range(tall) for dx in range(side)),
        key=lambda o: (reach(o[0], tall) + reach(o[1], side), o),
    )
    mirror = [offsets.index((-dy % tall, -dx % side)) for dy, dx in offsets]
    cuts = [0, 3 * C // 8, 3 * C // 4, C]
    group = [sum(j >= cut for cut in cuts[1:]) for j in range(C)]
    return side, tall, offsets, mirror, cuts, group


MSG, VAL, FINE, RED, HALO, COARSE = 0, 1, 2, 3, 5, 7
TO_MSG, TO_VAL, TO_FINE, TO_RED, TO_HALO, TO_COARSE = 0, 3, 6, 7, 9, 11


def kernel(
    R, C,
    amp_in, mask_in, leak_in, cleak_in, cinit_in, vf_in, vc_in, cnt_in,
    x_out, c_out,
    amp, mask, leak, cleak, cinit, vf, vc, cnt, load_sem,
    msg_out, msg_in, val_out, val_in, fval_out, fval_in,
    place_v, place_s, Bt, hot, dv, diag, V, rhs, W, G,
    ship, land,
    red_out, red_in, red2_out, red2_in,
    volt1, turn, seam_out, cland,
    send_sem, recv_sem,
):
    row, col = lax.axis_index("row"), lax.axis_index("col")
    sources_of = (cnt_in, vc_in, vf_in, cinit_in, leak_in, cleak_in, amp_in, mask_in)
    targets_of = (cnt, vc, vf, cinit, leak, cleak, amp, mask)
    loads = [
        pltpu.make_async_copy(source, target, load_sem.at[n])
        for n, (source, target) in enumerate(zip(sources_of, targets_of))
    ]
    for load in loads:
        load.start()
    TR, TC = leak.shape
    BR, BC = cleak.shape
    S = vf.shape[1]
    per = S // C
    up, down = lax.rem(row + R - 1, R), lax.rem(row + 1, R)
    left, right = lax.rem(col + C - 1, C), lax.rem(col + 1, C)
    side, tall, offsets, mirror, cuts, group = ring_order(C)
    col_y, col_x = col // side, col % side
    who = [
        lax.rem(col_y + dy, tall) * side + lax.rem(col_x + dx, side) for dy, dx in offsets
    ]

    barrier = pltpu.get_barrier_semaphore()
    peers = [(row, who[j]) for j in range(1, C)]
    peers += [(lax.rem(row + d, R), col) for d in range(1, R)]
    peers += [(u, s) for u in (up, down) for s in (left, right)]
    for peer in peers:
        pl.semaphore_signal(barrier, inc=1, device_id=peer, device_id_type=pl.DeviceIdType.MESH)

    def post(src, dst, device, phase, landing):
        pltpu.make_async_remote_copy(
            src_ref=src, dst_ref=dst, send_sem=send_sem.at[phase], recv_sem=recv_sem.at[landing],
            device_id=device, device_id_type=pl.DeviceIdType.MESH,
        ).start()

    def arrive(ref, landing):
        pltpu.make_async_copy(ref, ref, recv_sem.at[landing]).wait()

    def drain(ref, phase):
        pltpu.make_async_copy(ref, ref, send_sem.at[phase]).wait()

    def span(ref, g):
        first = max(cuts[g], 1)
        return ref.at[pl.ds(first, cuts[g + 1] - first)]

    def others(ref):
        return ref.at[pl.ds(1, C - 1)]

    def slots(ref, j):
        return ref[:, pl.ds(pl.multiple_of(who[j] * per, per), per)]

    loads[0].wait()
    loads[1].wait()
    lane = lax.broadcasted_iota(jnp.int32, (1, per), 1)
    for j in range(C):
        msg_out[j] = jnp.where(lane < cnt[0, who[j]], slots(vc, j), -1)
    msg_in[0] = msg_out[0]

    pl.semaphore_wait(barrier, len(peers))

    for j in reversed(range(1, C)):
        post(msg_out.at[j], msg_in.at[mirror[j]], (row, who[j]), MSG, TO_MSG + group[mirror[j]])

    def coarse_send(ref, n):
        phase, landing = COARSE + n, TO_COARSE + n
        post(ref.at[pl.ds(0, 8)], cland.at[n, pl.ds(0, 8)], (up, col), phase, landing)
        post(ref.at[pl.ds(BR - 8, 8)], cland.at[n, pl.ds(8, 8)], (down, col), phase, landing)
        post(seam_out.at[n, 0], cland.at[n, pl.ds(16, 8)], (row, left), phase, landing)
        post(seam_out.at[n, 1], cland.at[n, pl.ds(24, 8)], (row, right), phase, landing)

    groups = BC // GROUP

    def seams(volt, n):
        turn[n] = volt.T
        seam_out[n, 0] = turn[n, pl.ds(0, groups, stride=GROUP), :]
        seam_out[n, 1] = turn[n, pl.ds(GROUP - 1, groups, stride=GROUP), :]

    loads[2].wait()
    weight = jnp.concatenate(
        [jnp.where(lane < cnt[0, who[j]], via_conductance, 0.0).astype(F32) for j in range(C)],
        axis=1,
    )
    fine = jnp.concatenate([slots(vf, j) for j in range(C)], axis=1)
    fine_row = divide(fine, TC)
    fine_col = remainder(fine, TC)
    TE = TR + 32
    blocks = TC // LANES
    all_blocks = blocks + 1
    place_v[...] = (divide(fine_col, LANES) * TR + fine_row) * ITERS
    move = pltpu.make_async_copy(place_v, place_s, load_sem.at[8])
    move.start()
    lanes = lax.broadcasted_iota(jnp.int32, (per, TC), 1).astype(F32)
    for j in range(C):
        cut = slice(j * per, (j + 1) * per)
        turned = jnp.broadcast_to(fine_col[:, cut].astype(F32), (LANES, per)).T
        wide = jnp.concatenate([turned] * blocks, axis=1)
        Bt[cut, :] = jnp.where(wide == lanes, 1.0, 0.0).astype(BF16)

    loads[3].wait()
    seams(cinit[...], 0)
    coarse_send(cinit, 0)

    def ext(k, b, start, size):
        return pl.ds((k * all_blocks + b) * TE + start, size)

    def own(b, start, size):
        return pl.ds(b * TR + start, size)

    def part(b):
        return slice(b * LANES, (b + 1) * LANES)

    zero_pad = jnp.zeros((8, LANES), F32)
    for n in range(ITERS):
        for b in range(all_blocks):
            V[ext(n, b, 0, 8), :] = zero_pad
            V[ext(n, b, TR + 24, 8), :] = zero_pad

    loads[4].wait()
    wide_step = 256 if TR % 256 == 0 else 64

    def diagonal(i, carry):
        base = pl.multiple_of(i * wide_step, wide_step)
        place = lax.broadcasted_iota(jnp.int32, (wide_step, S), 0) + i * wide_step
        match = place == fine_row
        added = dot(jnp.where(match, weight, 0.0).astype(BF16), Bt[...])
        for b in range(blocks):
            value = 4.0 + leak[pl.ds(base, wide_step), part(b)] + added[:, part(b)]
            diag[own(b, base, wide_step), :] = value
            dv[ext(0, b, base + 16, wide_step), :] = 1.0 / value
        return carry

    lax.fori_loop(0, TR // wide_step, diagonal, 0)

    low_side = lax.broadcasted_iota(jnp.int32, (TR, LANES), 1) < LANES // 2
    quad = 8 * blocks

    def halo_send(F, n):
        phase, landing = HALO + n, TO_HALO + n
        sides = jnp.where(
            low_side, F[ext(0, 0, 16, TR), :], F[ext(0, blocks - 1, 16, TR), :]
        )
        turned = sides.T
        ship[n, 4 * quad : 4 * quad + 8, :] = sides[0:8]
        ship[n, 4 * quad + 8 : 4 * quad + 16, :] = sides[TR - 8 : TR]
        for b in range(TR // LANES):
            ship[n, 2 * quad + 8 * b : 2 * quad + 8 * b + 8, :] = turned[0:8, part(b)]
            ship[n, 3 * quad + 8 * b : 3 * quad + 8 * b + 8, :] = turned[LANES - 8 : LANES, part(b)]
        for b in range(blocks):
            ship[n, 8 * b : 8 * b + 8, :] = F[ext(0, b, 16, 8), :]
            ship[n, quad + 8 * b : quad + 8 * b + 8, :] = F[ext(0, b, TR + 8, 8), :]
        first, last = ship.at[n, pl.ds(4 * quad, 8)], ship.at[n, pl.ds(4 * quad + 8, 8)]
        for source, q, device in (
            (first, 3, (up, left)), (first, 2, (up, right)),
            (last, 1, (down, left)), (last, 0, (down, right)),
        ):
            post(source, land.at[n, pl.ds(4 * quad + 8 * q, 8)], device, phase, landing)
        for q, device in ((2, (row, left)), (3, (row, right)), (0, (up, col)), (1, (down, col))):
            at = pl.ds(q * quad, quad)
            post(ship.at[n, at], land.at[n, at], device, phase, landing)

    top_ok, bot_ok = row > 0, row < R - 1
    left_ok, right_ok = col > 0, col < C - 1

    def keep(ok, value):
        return value * jnp.where(ok, 1.0, 0.0).astype(F32)

    def halo_land(F, n):
        arrive(land.at[n], TO_HALO + n)
        for b in range(blocks):
            F[ext(0, b, 8, 8), :] = keep(top_ok, land[n, quad + 8 * b : quad + 8 * b + 8, :])
            F[ext(0, b, TR + 16, 8), :] = keep(bot_ok, land[n, 8 * b : 8 * b + 8, :])
        low, high = [
            jnp.concatenate(
                [
                    land[n, q * quad + 8 * b : q * quad + 8 * b + 8, :]
                    for b in range(TR // LANES)
                ], axis=1,
            )
            for q in (2, 3)
        ]
        strip = jnp.concatenate(
            [keep(right_ok, low), jnp.zeros((LANES - 16, TR), F32), keep(left_ok, high)], axis=0
        )
        F[ext(0, blocks, 16, TR), :] = strip.T
        low8 = lax.broadcasted_iota(jnp.int32, (8, LANES), 1)
        near_low, near_high = low8 < 8, low8 >= LANES - 8

        def corner(ok, lo, hi):
            lo = land[n, 4 * quad + 8 * lo : 4 * quad + 8 * lo + 8, :]
            hi = land[n, 4 * quad + 8 * hi : 4 * quad + 8 * hi + 8, :]
            return keep(
                ok,
                jnp.where(near_low, keep(right_ok, lo), 0.0)
                + jnp.where(near_high, keep(left_ok, hi), 0.0),
            )

        F[ext(0, blocks, 8, 8), :] = corner(top_ok, 1, 0)
        F[ext(0, blocks, TR + 16, 8), :] = corner(bot_ok, 3, 2)

    hi, lo = [piece.astype(BF16) for piece in halves(cinit[...])]
    place_r = lax.broadcasted_iota(jnp.int32, (BR, per), 0)
    place_c = lax.broadcasted_iota(jnp.int32, (BC, per), 0)
    for g in range(3):
        arrive(span(msg_in, g), TO_MSG + g)
        for p in range(cuts[g], cuts[g + 1]):
            cut = slice(p * per, (p + 1) * per)
            hot[:, cut] = jnp.where(place_c == remainder(msg_in[p], BC), 1.0, 0.0).astype(BF16)
        cut = slice(cuts[g] * per, cuts[g + 1] * per)
        glimpse = dot(hi, hot[:, cut]) + dot(lo, hot[:, cut])
        for p in range(cuts[g], cuts[g + 1]):
            at = (p - cuts[g]) * per
            here = jnp.where(place_r == divide(msg_in[p], BC * C), glimpse[:, at : at + per], 0.0)
            val_out[p] = jnp.sum(here, axis=0, keepdims=True)
        for p in reversed(range(max(cuts[g], 1), cuts[g + 1])):
            post(val_out.at[p], val_in.at[mirror[p]], (row, who[p]), VAL, TO_VAL + group[mirror[p]])
    val_in[0] = val_out[0]

    halo_send(dv, 0)

    def onto_coarse(amount):
        spread = jnp.concatenate(
            [
                jnp.where(place_r == divide(msg_in[p], BC * C), amount[p], 0.0).astype(BF16)
                for p in range(C)
            ], axis=1,
        )
        return lax.dot_general(
            spread, hot[...], (((1,), (1,)), ((), ())), preferred_element_type=F32
        )

    loads[5].wait()
    coarse_diag = 4.0 * coarse_conductance + cleak[...] + onto_coarse([via_conductance] * C)

    loads[6].wait()
    loads[7].wait()
    for g in range(3):
        arrive(span(val_in, g), TO_VAL + g)
        cut = slice(cuts[g] * per, cuts[g + 1] * per)
        heard = jnp.concatenate([val_in[p] for p in range(cuts[g], cuts[g + 1])], axis=1)
        drop_hi, drop_lo = halves(weight[:, cut] * heard)

        def inject(i, carry, g=g, cut=cut, drop_hi=drop_hi, drop_lo=drop_lo):
            base = pl.multiple_of(i * wide_step, wide_step)
            place = lax.broadcasted_iota(jnp.int32, (wide_step, cut.stop - cut.start), 0) + base
            match = place == fine_row[:, cut]
            both = [jnp.where(match, piece, 0.0).astype(BF16) for piece in (drop_hi, drop_lo)]
            both = dot(jnp.concatenate(both, axis=0), Bt[cut, :])
            added = both[:wide_step] + both[wide_step:]
            at = pl.ds(base, wide_step)
            for b in range(blocks):
                if g == 0:
                    value = amp[at, part(b)] * mask[at, part(b)].astype(F32) + added[:, part(b)]
                else:
                    value = rhs[own(b, base, wide_step), :] + added[:, part(b)]
                rhs[own(b, base, wide_step), :] = value
                if g == 2:
                    inner = ext(0, b, base + 16, wide_step)
                    V[inner, :] = value * dv[inner, :]
            return carry

        lax.fori_loop(0, TR // wide_step, inject, 0)
    halo_send(V, 1)
    halo_land(dv, 0)
    halo_land(V, 1)

    rows = chunk_of(TR + 16, 176)

    def around(k, start, size, count):
        first = lax.broadcasted_iota(jnp.int32, (size, LANES), 1) == 0
        last = lax.broadcasted_iota(jnp.int32, (size, LANES), 1) == LANES - 1
        mid = [V[ext(k, b, start, size), :] for b in range(all_blocks)]
        after = [pltpu.roll(m, LANES - 1, 1) for m in mid]
        before = [pltpu.roll(m, 1, 1) for m in mid]
        found = []
        for b in range(count):
            tall = V[ext(k, b, start - 1, size), :] + V[ext(k, b, start + 1, size), :]
            left_of = jnp.where(first, before[b - 1], before[b])
            right_of = jnp.where(last, after[(b + 1) % all_blocks], after[b])
            found.append(tall + (left_of + right_of))
        return mid, found

    for k in range(ITERS - 1):

        def advance(i, carry, k=k):
            start = pl.multiple_of(8 + i * rows, 8)
            near = around(k, start, rows, all_blocks)[1]
            for b in range(all_blocks):
                fresh = dv[ext(0, b, start, rows), :] * near[b]
                if k:
                    fresh = (fresh + fresh) - V[ext(k - 1, b, start, rows), :]
                V[ext(k + 1, b, start, rows), :] = fresh
            return carry

        lax.fori_loop(0, (TR + 16) // rows, advance, 0)

    orders = 2 * ITERS - 1
    sums = orders + ITERS
    tall_step = 64

    def fold(value):
        total = value[0:8]
        for n in range(1, tall_step // 8):
            total = total + value[n * 8 : n * 8 + 8]
        return total

    def gram(i, carry):
        base = pl.multiple_of(i * tall_step, tall_step)
        mid, near = around(ITERS - 1, base + 16, tall_step, blocks)
        totals = list(carry)
        for b in range(blocks):
            at = own(b, base, tall_step)
            v = [V[ext(k, b, base + 16, tall_step), :] for k in range(ITERS - 1)] + [mid[b]]
            source, held = rhs[at, :], diag[at, :]
            low, high = held * (v[0] - v[1]), held * mid[b] - near[b]
            for k in range(ITERS):
                W[pl.ds((b * TR + base) * ITERS + k, tall_step, stride=ITERS), :] = v[k]
            fresh = [fold(low * v[k]) for k in range(ITERS)]
            fresh += [fold(high * v[k]) for k in range(1, ITERS)]
            fresh += [fold(source * v[k]) for k in range(ITERS)]
            totals = [x + y for x, y in zip(totals, fresh)]
        return tuple(totals)

    totals = lax.fori_loop(
        0, TR // tall_step, gram, tuple(jnp.zeros((8, LANES), F32) for _ in range(sums))
    )
    flat = jnp.concatenate(
        [jnp.sum(total, axis=0, keepdims=True) for total in totals]
        + [jnp.zeros((16 - sums, LANES), F32)], axis=0,
    )
    same = lax.broadcasted_iota(jnp.int32, (16, LANES), 0) == lax.broadcasted_iota(
        jnp.int32, (16, LANES), 1
    )
    number = jnp.sum(flat, axis=1, keepdims=True)
    red_out[...] = jnp.sum(jnp.where(same, number, 0.0), axis=0, keepdims=True)
    red_in[0] = red_out[...]
    for j in reversed(range(1, C)):
        post(red_out, red_in.at[mirror[j]], (row, who[j]), RED, TO_RED)

    move.wait()
    reach = 32

    def fetch(i, carry):
        for j in range(reach):
            s = i * reach + j
            G[pl.ds(s * ITERS, ITERS), :] = W[pl.ds(place_s[0, s], ITERS), :]
        return carry

    lax.fori_loop(0, S // reach, fetch, 0)
    turned_lane = lax.broadcasted_iota(jnp.int32, (LANES, per), 0)
    fine_lane = remainder(fine_col, LANES)
    for j in reversed(range(C)):
        pick = turned_lane == fine_lane[:, j * per : (j + 1) * per]
        for k in range(ITERS):
            turned = G[pl.ds(j * per * ITERS + k, per, stride=ITERS), :].T
            fval_out[j, k : k + 1, :] = jnp.sum(jnp.where(pick, turned, 0.0), axis=0, keepdims=True)
    for j in reversed(range(1, C)):
        post(fval_out.at[j], fval_in.at[mirror[j]], (row, who[j]), FINE, TO_FINE)
    fval_in[0] = fval_out[0]

    place = lax.broadcasted_iota(jnp.int32, (BR, BC), 1)
    place_u = lax.broadcasted_iota(jnp.int32, (BR, BC), 0)
    within = remainder(place, GROUP)

    def beside(volt, n):
        above = jnp.where(place_u == 0, keep(top_ok, cland[n, 15:16, :]), pltpu.roll(volt, 1, 0))
        below = jnp.where(
            place_u == BR - 1, keep(bot_ok, cland[n, 0:1, :]), pltpu.roll(volt, BR - 1, 0)
        )
        group_at = lax.broadcasted_iota(jnp.int32, (groups, BR), 0)
        far = cland[n, 24:32, :]
        turn[n, pl.ds(0, groups, stride=GROUP), :] = jnp.where(
            left_ok, far, jnp.where(group_at == 0, 0.0, jnp.roll(far, 1, 0))
        )
        far = cland[n, 16:24, :]
        turn[n, pl.ds(GROUP - 1, groups, stride=GROUP), :] = jnp.where(
            right_ok, far, jnp.where(group_at == groups - 1, 0.0, jnp.roll(far, -1, 0))
        )
        edge = turn[n].T
        before = jnp.where(within == 0, edge, pltpu.roll(volt, 1, 1))
        after = jnp.where(within == GROUP - 1, edge, pltpu.roll(volt, BC - 1, 1))
        return above + below + before + after

    arrive(cland.at[0], TO_COARSE)
    volt = cinit[...]
    scale = relaxation / coarse_diag
    partial = volt + scale * (coarse_conductance * beside(volt, 0) - coarse_diag * volt)

    arrive(others(red_in), TO_RED)
    total = red_in[0]
    for j in range(1, C):
        total = total + red_in[j]
    red2_out[...] = total
    for d in range(1, R):
        post(red2_out, red2_in.at[d - 1], (lax.rem(row + d, R), col), RED + 1, TO_RED + 1)
    arrive(red2_in, TO_RED + 1)
    for d in range(R - 1):
        total = total + red2_in[d]
    number = jnp.sum(jnp.where(same, jnp.broadcast_to(total, (16, LANES)), 0.0), axis=1, keepdims=True)
    number = [number[n : n + 1, :] for n in range(sums)]

    matrix = [[None] * (ITERS + 1) for _ in range(ITERS)]
    for n in range(ITERS, orders):
        number[n] = 2.0 * number[n] - number[2 * (ITERS - 1) - n]
    for j in range(ITERS):
        for k in range(j + 1):
            matrix[j][k] = matrix[k][j] = 0.5 * (number[j + k] + number[j - k])
        matrix[j][ITERS] = number[orders + j]
    for i in range(ITERS):
        inverse = 1.0 / matrix[i][i]
        for k in range(i + 1, ITERS + 1):
            matrix[i][k] = matrix[i][k] * inverse
        for j in range(i + 1, ITERS):
            for k in range(i + 1, ITERS + 1):
                matrix[j][k] = matrix[j][k] - matrix[j][i] * matrix[i][k]
    coef = [None] * ITERS
    for i in reversed(range(ITERS)):
        coef[i] = matrix[i][ITERS]
        for k in range(i + 1, ITERS):
            coef[i] = coef[i] - matrix[i][k] * coef[k]

    arrive(others(fval_in), TO_FINE)
    amount = []
    for p in range(C):
        found = coef[0] * fval_in[p, 0:1, :]
        for k in range(1, ITERS):
            found = found + coef[k] * fval_in[p, k : k + 1, :]
        amount.append(halves(via_conductance * found))
    sources = onto_coarse([a[0] for a in amount]) + onto_coarse([a[1] for a in amount])
    volt = partial + scale * sources
    volt1[...] = volt
    seams(volt, 1)
    coarse_send(volt1, 1)
    partial = volt + scale * (sources - coarse_diag * volt)
    step = 64

    def finish(i, carry):
        base = pl.multiple_of(i * step, step)
        for b in range(blocks):
            value = coef[0] * V[ext(0, b, base + 16, step), :]
            for k in range(1, ITERS):
                value = value + coef[k] * V[ext(k, b, base + 16, step), :]
            x_out[pl.ds(base, step), part(b)] = value
        return carry

    lax.fori_loop(0, TR // step, finish, 0)
    drain(others(msg_out), MSG)
    drain(others(val_out), VAL)
    drain(others(fval_out), FINE)
    drain(others(red_in), RED)
    drain(red2_in, RED + 1)
    for n in range(2):
        drain(land.at[n], HALO + n)
        drain(cland.at[n], COARSE + n)
    arrive(cland.at[1], TO_COARSE + 1)
    c_out[...] = partial + scale * (coarse_conductance * beside(volt, 1))


def per_device(R, C, load_amp, load_mask, leak, coarse_leak, coarse_init, via_fine, via_coarse, via_count):
    TR, TC = leak.shape
    BR, BC = coarse_leak.shape
    S = via_fine.shape[1]
    per = S // C
    vmem = pl.BlockSpec(memory_space=pltpu.VMEM)
    blocks = TC // LANES
    ext = (blocks + 1) * (TR + 32)
    return pl.pallas_call(
        functools.partial(kernel, R, C),
        out_shape=(pltpu.VMEM((TR, TC), F32), pltpu.VMEM((BR, BC), F32)),
        in_specs=[pl.BlockSpec(memory_space=pltpu.HBM)] * 8,
        out_specs=(vmem, vmem),
        scratch_shapes=[
            pltpu.VMEM((TR, TC), F32), pltpu.VMEM((TR, TC), jnp.int32), pltpu.VMEM((TR, TC), F32),
            pltpu.VMEM((BR, BC), F32), pltpu.VMEM((BR, BC), F32),
            pltpu.VMEM((1, S), jnp.int32), pltpu.VMEM((1, S), jnp.int32),
            pltpu.SMEM((1, C), jnp.int32), pltpu.SemaphoreType.DMA((9,)),
            pltpu.VMEM((C, 1, per), jnp.int32), pltpu.VMEM((C, 1, per), jnp.int32),
            pltpu.VMEM((C, 1, per), F32), pltpu.VMEM((C, 1, per), F32),
            pltpu.VMEM((C, ITERS, per), F32), pltpu.VMEM((C, ITERS, per), F32),
            pltpu.VMEM((1, S), jnp.int32), pltpu.SMEM((1, S), jnp.int32),
            pltpu.VMEM((S, TC), BF16),
            pltpu.VMEM((BC, S), BF16),
            pltpu.VMEM((ext, LANES), F32),
            pltpu.VMEM((blocks * TR, LANES), F32),
            pltpu.VMEM((ITERS * ext, LANES), F32),
            pltpu.VMEM((blocks * TR, LANES), F32),
            pltpu.VMEM((ITERS * blocks * TR, LANES), F32),
            pltpu.VMEM((ITERS * S, LANES), F32),
            pltpu.VMEM((2, 32 * blocks + 16, LANES), F32),
            pltpu.VMEM((2, 32 * blocks + 32, LANES), F32),
            pltpu.VMEM((1, LANES), F32), pltpu.VMEM((C, 1, LANES), F32),
            pltpu.VMEM((1, LANES), F32), pltpu.VMEM((R - 1, 1, LANES), F32),
            pltpu.VMEM((BR, BC), F32),
            pltpu.VMEM((2, BC, BR), F32), pltpu.VMEM((2, 2, BC // GROUP, BR), F32),
            pltpu.VMEM((2, 32, BC), F32),
            pltpu.SemaphoreType.DMA((9,)),
            pltpu.SemaphoreType.DMA((13,)),
        ],
        compiler_params=pltpu.CompilerParams(
            collective_id=0, has_side_effects=True, vmem_limit_bytes=60 * 1024 * 1024
        ),
    )(load_amp, load_mask, leak, coarse_leak, coarse_init, via_fine, via_coarse, via_count)


def solution(mesh):
    spec = P("row", "col")
    return jax.shard_map(
        functools.partial(per_device, mesh.shape["row"], mesh.shape["col"]),
        mesh=mesh, in_specs=(spec,) * 8, out_specs=(spec, spec), check_vma=False,
    )
```

time: 52.6 us -> 44.2 us (0.84)
  Pallas kernels: 50.3 us -> 41.7 us
    pallas_call x1, Pallas kernels: 50.3 us -> 41.7 us  [per_device(): pl.pallas_call(functools.partial(kernel, R, C), out_shape=(pltpu.VMEM((TR...]
where the time goes in v2:
time: 44.2 us; the launch traced here: 43.9 us
  Pallas kernels  41.7 us (94%)
  local copies, waits for them, and re-layouts  1.6 us (4%)
  between operations  0.64 us (1%)
    pallas_call x1, Pallas kernels, per_device(): pl.pallas_call(functools.partial(kernel, R, C), out_shape=(pltpu.VMEM((TR...  41.7 us
    unnamed x2, local copies, waits for them, and re-layouts  1.6 us

profile of v2, /device:TPU:0, one launch (start us, length us, event | category | flops | bytes accessed | tf_op | source)
XLA Modules:
  0.0 43.9 jit_solution(235516464349024140)
XLA Ops:
  0.6 41.7 %shard_map.95 = (f32[512,512]{1,0:T(8,128)S(1)}, f32[128,128]{1,0:T(8,128)S(1)}) custom-call(f32[512,512]{1,0:T(8,128)} %amp_in.1, s32[512,512]{1,0:T(8,128)} %mask_in.1, f32[512,512]{1,0:T(8,128)} %leak_in.1, f32[128,128]{1,0:T(8,128)} %cleak_in.1, f32[128,128]{1,0:T(8,128)} %cinit_in.1, s32[1,2048]{1,0:T(1,128)} %vf_in.1, s32[1,2048]{1,0:T(1,128)} %vc_in.1, ...), custom_call_target="tpu_custom_call" | custom-call | tf_op jit(solution)/shard_map/pallas_call | solution.py:546
  42.3 1.0 %copy.12 = f32[512,512]{1,0:T(8,128)} copy(f32[512,512]{1,0:T(8,128)S(1)} %get-tuple-element.2) | data formatting | bytes 2097152
  43.3 0.6 %copy.13 = f32[128,128]{1,0:T(8,128)} copy(f32[128,128]{1,0:T(8,128)S(1)} %get-tuple-element.3) | data formatting | bytes 131072

commit v3 on v2

--- a/solution.py
+++ b/solution.py
@@ -75,9 +75,9 @@
     msg_out, msg_in, val_out, val_in, fval_out, fval_in,
     place_v, place_s, Bt, hot, dv, diag, V, rhs, W, G,
     ship, land,
-    red_out, red_in, red2_out, red2_in,
+    red_out, red_in,
     volt1, turn, seam_out, cland,
-    send_sem, recv_sem,
+    send_sem, recv_sem, ready,
 ):
     row, col = lax.axis_index("row"), lax.axis_index("col")
     sources_of = (cnt_in, vc_in, vf_in, cinit_in, leak_in, cleak_in, amp_in, mask_in)
@@ -294,6 +294,11 @@
         for p in reversed(range(max(cuts[g], 1), cuts[g + 1])):
             post(val_out.at[p], val_in.at[mirror[p]], (row, who[p]), VAL, TO_VAL + group[mirror[p]])
     val_in[0] = val_out[0]
+    for d in range(1, R):
+        pl.semaphore_signal(
+            ready, inc=1, device_id=(lax.rem(row + d, R), col),
+            device_id_type=pl.DeviceIdType.MESH,
+        )
 
     halo_send(dv, 0)
 
@@ -413,28 +418,36 @@
     number = jnp.sum(flat, axis=1, keepdims=True)
     red_out[...] = jnp.sum(jnp.where(same, number, 0.0), axis=0, keepdims=True)
     red_in[0] = red_out[...]
-    for j in reversed(range(1, C)):
-        post(red_out, red_in.at[mirror[j]], (row, who[j]), RED, TO_RED)
+    pl.semaphore_wait(ready, R - 1)
+    for d in sorted(range(R), key=lambda d: -min(d, R - d)):
+        for j in reversed(range(C)):
+            if d or j:
+                slot = (R - d) % R * C + mirror[j]
+                post(red_out, red_in.at[slot], (lax.rem(row + d, R), who[j]), RED, TO_RED)
 
     move.wait()
-    reach = 32
-
-    def fetch(i, carry):
-        for j in range(reach):
-            s = i * reach + j
-            G[pl.ds(s * ITERS, ITERS), :] = W[pl.ds(place_s[0, s], ITERS), :]
-        return carry
-
-    lax.fori_loop(0, S // reach, fetch, 0)
+    reach = 64
     turned_lane = lax.broadcasted_iota(jnp.int32, (LANES, per), 0)
     fine_lane = remainder(fine_col, LANES)
-    for j in reversed(range(C)):
-        pick = turned_lane == fine_lane[:, j * per : (j + 1) * per]
-        for k in range(ITERS):
-            turned = G[pl.ds(j * per * ITERS + k, per, stride=ITERS), :].T
-            fval_out[j, k : k + 1, :] = jnp.sum(jnp.where(pick, turned, 0.0), axis=0, keepdims=True)
-    for j in reversed(range(1, C)):
-        post(fval_out.at[j], fval_in.at[mirror[j]], (row, who[j]), FINE, TO_FINE)
+    flock = max(C // 4, 1)
+    for first in reversed(range(0, C, flock)):
+
+        def fetch(i, carry, first=first):
+            for j in range(reach):
+                s = first * per + i * reach + j
+                G[pl.ds(s * ITERS, ITERS), :] = W[pl.ds(place_s[0, s], ITERS), :]
+            return carry
+
+        lax.fori_loop(0, flock * per // reach, fetch, 0)
+        for j in reversed(range(first, first + flock)):
+            pick = turned_lane == fine_lane[:, j * per : (j + 1) * per]
+            for k in range(ITERS):
+                turned = G[pl.ds(j * per * ITERS + k, per, stride=ITERS), :].T
+                fval_out[j, k : k + 1, :] = jnp.sum(
+                    jnp.where(pick, turned, 0.0), axis=0, keepdims=True
+                )
+        for j in reversed(range(max(first, 1), first + flock)):
+            post(fval_out.at[j], fval_in.at[mirror[j]], (row, who[j]), FINE, TO_FINE)
     fval_in[0] = fval_out[0]
 
     place = lax.broadcasted_iota(jnp.int32, (BR, BC), 1)
@@ -465,16 +478,8 @@
     scale = relaxation / coarse_diag
     partial = volt + scale * (coarse_conductance * beside(volt, 0) - coarse_diag * volt)
 
-    arrive(others(red_in), TO_RED)
-    total = red_in[0]
-    for j in range(1, C):
-        total = total + red_in[j]
-    red2_out[...] = total
-    for d in range(1, R):
-        post(red2_out, red2_in.at[d - 1], (lax.rem(row + d, R), col), RED + 1, TO_RED + 1)
-    arrive(red2_in, TO_RED + 1)
-    for d in range(R - 1):
-        total = total + red2_in[d]
+    arrive(red_in.at[pl.ds(1, R * C - 1)], TO_RED)
+    total = jnp.sum(red_in[...], axis=0)
     number = jnp.sum(jnp.where(same, jnp.broadcast_to(total, (16, LANES)), 0.0), axis=1, keepdims=True)
     number = [number[n : n + 1, :] for n in range(sums)]
 
@@ -526,8 +531,7 @@
     drain(others(msg_out), MSG)
     drain(others(val_out), VAL)
     drain(others(fval_out), FINE)
-    drain(others(red_in), RED)
-    drain(red2_in, RED + 1)
+    drain(red_in.at[pl.ds(1, R * C - 1)], RED)
     for n in range(2):
         drain(land.at[n], HALO + n)
         drain(cland.at[n], COARSE + n)
@@ -567,13 +571,13 @@
             pltpu.VMEM((ITERS * S, LANES), F32),
             pltpu.VMEM((2, 32 * blocks + 16, LANES), F32),
             pltpu.VMEM((2, 32 * blocks + 32, LANES), F32),
-            pltpu.VMEM((1, LANES), F32), pltpu.VMEM((C, 1, LANES), F32),
-            pltpu.VMEM((1, LANES), F32), pltpu.VMEM((R - 1, 1, LANES), F32),
+            pltpu.VMEM((1, LANES), F32), pltpu.VMEM((R * C, 1, LANES), F32),
             pltpu.VMEM((BR, BC), F32),
             pltpu.VMEM((2, BC, BR), F32), pltpu.VMEM((2, 2, BC // GROUP, BR), F32),
             pltpu.VMEM((2, 32, BC), F32),
             pltpu.SemaphoreType.DMA((9,)),
             pltpu.SemaphoreType.DMA((13,)),
+            pltpu.SemaphoreType.REGULAR,
         ],
         compiler_params=pltpu.CompilerParams(
             collective_id=0, has_side_effects=True, vmem_limit_bytes=60 * 1024 * 1024

time: 44.2 us -> 43.3 us (0.980)
  Pallas kernels: 41.7 us -> 40.9 us
    pallas_call x1, Pallas kernels: 41.7 us -> 40.9 us  [per_device(): pl.pallas_call(functools.partial(kernel, R, C), out_shape=(pltpu.VMEM((TR...]
where the time goes in v3:
time: 43.3 us; the launch traced here: 43.1 us
  Pallas kernels  40.9 us (94%)
  local copies, waits for them, and re-layouts  1.6 us (4%)
  between operations  0.64 us (1%)
    pallas_call x1, Pallas kernels, per_device(): pl.pallas_call(functools.partial(kernel, R, C), out_shape=(pltpu.VMEM((TR...  40.9 us
    unnamed x2, local copies, waits for them, and re-layouts  1.6 us

profile of v3, /device:TPU:0, one launch (start us, length us, event | category | flops | bytes accessed | tf_op | source)
XLA Modules:
  0.0 43.1 jit_solution(10282650966299133983)
XLA Ops:
  0.6 40.9 %shard_map.95 = (f32[512,512]{1,0:T(8,128)S(1)}, f32[128,128]{1,0:T(8,128)S(1)}) custom-call(f32[512,512]{1,0:T(8,128)} %amp_in.1, s32[512,512]{1,0:T(8,128)} %mask_in.1, f32[512,512]{1,0:T(8,128)} %leak_in.1, f32[128,128]{1,0:T(8,128)} %cleak_in.1, f32[128,128]{1,0:T(8,128)} %cinit_in.1, s32[1,2048]{1,0:T(1,128)} %vf_in.1, s32[1,2048]{1,0:T(1,128)} %vc_in.1, ...), custom_call_target="tpu_custom_call" | custom-call | tf_op jit(solution)/shard_map/pallas_call | solution.py:550
  41.5 1.0 %copy.12 = f32[512,512]{1,0:T(8,128)} copy(f32[512,512]{1,0:T(8,128)S(1)} %get-tuple-element.2) | data formatting | bytes 2097152
  42.5 0.6 %copy.13 = f32[128,128]{1,0:T(8,128)} copy(f32[128,128]{1,0:T(8,128)S(1)} %get-tuple-element.3) | data formatting | bytes 131072

commit v4 on v3

--- a/solution.py
+++ b/solution.py
@@ -73,7 +73,7 @@
     x_out, c_out,
     amp, mask, leak, cleak, cinit, vf, vc, cnt, load_sem,
     msg_out, msg_in, val_out, val_in, fval_out, fval_in,
-    place_v, place_s, Bt, hot, dv, diag, V, rhs, W, G,
+    place_v, place_s, Bt, hot, dv, diag, V, rhs, W, G, side_dv, side_v,
     ship, land,
     red_out, red_in,
     volt1, turn, seam_out, cland,
@@ -194,6 +194,8 @@
         for b in range(all_blocks):
             V[ext(n, b, 0, 8), :] = zero_pad
             V[ext(n, b, TR + 24, 8), :] = zero_pad
+        side_v[pl.ds(n * TE, 8), :] = zero_pad
+        side_v[pl.ds(n * TE + TR + 24, 8), :] = zero_pad
 
     loads[4].wait()
     wide_step = 256 if TR % 256 == 0 else 64
@@ -346,68 +348,136 @@
         lax.fori_loop(0, TR // wide_step, inject, 0)
     halo_send(V, 1)
     halo_land(dv, 0)
-    halo_land(V, 1)
-
-    rows = chunk_of(TR + 16, 176)
-
-    def around(k, start, size, count):
+
+    def near_of(k, start, size, wanted, closed=True):
         first = lax.broadcasted_iota(jnp.int32, (size, LANES), 1) == 0
         last = lax.broadcasted_iota(jnp.int32, (size, LANES), 1) == LANES - 1
-        mid = [V[ext(k, b, start, size), :] for b in range(all_blocks)]
-        after = [pltpu.roll(m, LANES - 1, 1) for m in mid]
-        before = [pltpu.roll(m, 1, 1) for m in mid]
-        found = []
-        for b in range(count):
+        mid, before, after = {}, {}, {}
+        for b in wanted:
+            for near in (b - 1, b, b + 1):
+                near = near % all_blocks
+                if near not in mid and (closed or near < blocks):
+                    mid[near] = V[ext(k, near, start, size), :]
+        for b in mid:
+            before[b] = pltpu.roll(mid[b], 1, 1)
+            after[b] = pltpu.roll(mid[b], LANES - 1, 1)
+        found = {}
+        for b in wanted:
             tall = V[ext(k, b, start - 1, size), :] + V[ext(k, b, start + 1, size), :]
-            left_of = jnp.where(first, before[b - 1], before[b])
-            right_of = jnp.where(last, after[(b + 1) % all_blocks], after[b])
-            found.append(tall + (left_of + right_of))
+            left_of, right_of = before[b], after[b]
+            if closed or b:
+                left_of = jnp.where(first, before[(b - 1) % all_blocks], left_of)
+            if closed or b < blocks - 1:
+                right_of = jnp.where(last, after[(b + 1) % all_blocks], right_of)
+            found[b] = tall + (left_of + right_of)
         return mid, found
 
+    def forward(k, start, size, wanted, closed=True):
+        near = near_of(k, start, size, wanted, closed)[1]
+        for b in wanted:
+            fresh = dv[ext(0, b, start, size), :] * near[b]
+            if k:
+                fresh = (fresh + fresh) - V[ext(k - 1, b, start, size), :]
+            V[ext(k + 1, b, start, size), :] = fresh
+
+    core_rows = chunk_of(TR, 128)
     for k in range(ITERS - 1):
 
-        def advance(i, carry, k=k):
-            start = pl.multiple_of(8 + i * rows, 8)
-            near = around(k, start, rows, all_blocks)[1]
-            for b in range(all_blocks):
-                fresh = dv[ext(0, b, start, rows), :] * near[b]
-                if k:
-                    fresh = (fresh + fresh) - V[ext(k - 1, b, start, rows), :]
-                V[ext(k + 1, b, start, rows), :] = fresh
+        def inside(i, carry, k=k):
+            start = pl.multiple_of(16 + i * core_rows, 8)
+            forward(k, start, core_rows, range(blocks), False)
             return carry
 
-        lax.fori_loop(0, (TR + 16) // rows, advance, 0)
+        lax.fori_loop(0, TR // core_rows, inside, 0)
 
     orders = 2 * ITERS - 1
     sums = orders + ITERS
-    tall_step = 64
 
     def fold(value):
         total = value[0:8]
-        for n in range(1, tall_step // 8):
+        for n in range(1, value.shape[0] // 8):
             total = total + value[n * 8 : n * 8 + 8]
         return total
 
-    def gram(i, carry):
-        base = pl.multiple_of(i * tall_step, tall_step)
-        mid, near = around(ITERS - 1, base + 16, tall_step, blocks)
-        totals = list(carry)
-        for b in range(blocks):
-            at = own(b, base, tall_step)
-            v = [V[ext(k, b, base + 16, tall_step), :] for k in range(ITERS - 1)] + [mid[b]]
+    def gram(start, size, wanted, totals):
+        mid, near = near_of(ITERS - 1, start, size, wanted)
+        totals = list(totals)
+        for b in wanted:
+            at = own(b, start - 16, size)
+            v = [V[ext(k, b, start, size), :] for k in range(ITERS - 1)] + [mid[b]]
             source, held = rhs[at, :], diag[at, :]
             low, high = held * (v[0] - v[1]), held * mid[b] - near[b]
             for k in range(ITERS):
-                W[pl.ds((b * TR + base) * ITERS + k, tall_step, stride=ITERS), :] = v[k]
+                W[pl.ds((b * TR + start - 16) * ITERS + k, size, stride=ITERS), :] = v[k]
             fresh = [fold(low * v[k]) for k in range(ITERS)]
             fresh += [fold(high * v[k]) for k in range(1, ITERS)]
             fresh += [fold(source * v[k]) for k in range(ITERS)]
             totals = [x + y for x, y in zip(totals, fresh)]
         return tuple(totals)
 
-    totals = lax.fori_loop(
-        0, TR // tall_step, gram, tuple(jnp.zeros((8, LANES), F32) for _ in range(sums))
+    tall_step = 64
+    full = (TR - 16) // tall_step
+    rest = TR - 16 - full * tall_step
+
+    def middle(wanted, totals):
+        def body(i, carry):
+            return gram(pl.multiple_of(24 + i * tall_step, 8), tall_step, wanted, carry)
+
+        totals = lax.fori_loop(0, full, body, totals)
+        if rest:
+            totals = gram(24 + full * tall_step, rest, wanted, totals)
+        return totals
+
+    totals = middle(range(1, blocks - 1), tuple(jnp.zeros((8, LANES), F32) for _ in range(sums)))
+
+    rows = chunk_of(TR + 16, 176)
+
+    def low_half(size):
+        return lax.broadcasted_iota(jnp.int32, (size, LANES), 1) < LANES // 2
+
+    side_dv[8 : TR + 24, :] = jnp.where(
+        low_half(TR + 16), dv[ext(0, 0, 8, TR + 16), :], dv[ext(0, blocks - 1, 8, TR + 16), :]
     )
+    halo_land(V, 1)
+    side_v[8 : TR + 24, :] = jnp.where(
+        low_half(TR + 16), V[ext(0, 0, 8, TR + 16), :], V[ext(0, blocks - 1, 8, TR + 16), :]
+    )
+    for k in range(ITERS - 1):
+        for start in (8, TR + 8):
+            forward(k, start, 16, range(blocks))
+
+        def strips(i, carry, k=k):
+            start = pl.multiple_of(8 + i * rows, 8)
+            spot = lax.broadcasted_iota(jnp.int32, (rows, LANES), 1)
+            first, last = spot == 0, spot == LANES - 1
+            inner, outer = side_v[pl.ds(k * TE + start, rows), :], V[ext(k, blocks, start, rows), :]
+            inner_left, inner_right = pltpu.roll(inner, 1, 1), pltpu.roll(inner, LANES - 1, 1)
+            outer_left, outer_right = pltpu.roll(outer, 1, 1), pltpu.roll(outer, LANES - 1, 1)
+            near = side_v[pl.ds(k * TE + start - 1, rows), :] + side_v[pl.ds(k * TE + start + 1, rows), :]
+            near = near + (
+                jnp.where(first, outer_left, inner_left) + jnp.where(last, outer_right, inner_right)
+            )
+            fresh = side_dv[pl.ds(start, rows), :] * near
+            if k:
+                fresh = (fresh + fresh) - side_v[pl.ds((k - 1) * TE + start, rows), :]
+            side_v[pl.ds((k + 1) * TE + start, rows), :] = fresh
+            pltpu.store(V.at[ext(k + 1, 0, start, rows), :], fresh, mask=spot < 8)
+            pltpu.store(V.at[ext(k + 1, blocks - 1, start, rows), :], fresh, mask=spot >= LANES - 8)
+            near = V[ext(k, blocks, start - 1, rows), :] + V[ext(k, blocks, start + 1, rows), :]
+            near = near + (
+                jnp.where(first, inner_left, outer_left) + jnp.where(last, inner_right, outer_right)
+            )
+            fresh = dv[ext(0, blocks, start, rows), :] * near
+            if k:
+                fresh = (fresh + fresh) - V[ext(k - 1, blocks, start, rows), :]
+            V[ext(k + 1, blocks, start, rows), :] = fresh
+            return carry
+
+        lax.fori_loop(0, (TR + 16) // rows, strips, 0)
+
+    for start in (16, TR + 8):
+        totals = gram(start, 8, range(blocks), totals)
+    totals = middle((0, blocks - 1), totals)
     flat = jnp.concatenate(
         [jnp.sum(total, axis=0, keepdims=True) for total in totals]
         + [jnp.zeros((16 - sums, LANES), F32)], axis=0,
@@ -569,6 +639,7 @@
             pltpu.VMEM((blocks * TR, LANES), F32),
             pltpu.VMEM((ITERS * blocks * TR, LANES), F32),
             pltpu.VMEM((ITERS * S, LANES), F32),
+            pltpu.VMEM((TR + 32, LANES), F32), pltpu.VMEM((ITERS * (TR + 32), LANES), F32),
             pltpu.VMEM((2, 32 * blocks + 16, LANES), F32),
             pltpu.VMEM((2, 32 * blocks + 32, LANES), F32),
             pltpu.VMEM((1, LANES), F32), pltpu.VMEM((R * C, 1, LANES), F32),

time: 43.3 us -> 41.7 us (0.963)
  Pallas kernels: 40.9 us -> 39.4 us
    pallas_call x1, Pallas kernels: 40.9 us -> 39.4 us  [per_device(): pl.pallas_call(functools.partial(kernel, R, C), out_shape=(pltpu.VMEM((TR...]
where the time goes in v4:
time: 41.7 us; the launch traced here: 41.6 us
  Pallas kernels  39.4 us (94%)
  local copies, waits for them, and re-layouts  1.6 us (4%)
  between operations  0.64 us (2%)
    pallas_call x1, Pallas kernels, per_device(): pl.pallas_call(functools.partial(kernel, R, C), out_shape=(pltpu.VMEM((TR...  39.4 us
    unnamed x2, local copies, waits for them, and re-layouts  1.6 us

profile of v4, /device:TPU:0, one launch (start us, length us, event | category | flops | bytes accessed | tf_op | source)
XLA Modules:
  0.0 41.6 jit_solution(11411015505227254796)
XLA Ops:
  0.6 39.4 %shard_map.95 = (f32[512,512]{1,0:T(8,128)S(1)}, f32[128,128]{1,0:T(8,128)S(1)}) custom-call(f32[512,512]{1,0:T(8,128)} %amp_in.1, s32[512,512]{1,0:T(8,128)} %mask_in.1, f32[512,512]{1,0:T(8,128)} %leak_in.1, f32[128,128]{1,0:T(8,128)} %cleak_in.1, f32[128,128]{1,0:T(8,128)} %cinit_in.1, s32[1,2048]{1,0:T(1,128)} %vf_in.1, s32[1,2048]{1,0:T(1,128)} %vc_in.1, ...), custom_call_target="tpu_custom_call" | custom-call | tf_op jit(solution)/shard_map/pallas_call | solution.py:620
  40.0 1.0 %copy.12 = f32[512,512]{1,0:T(8,128)} copy(f32[512,512]{1,0:T(8,128)S(1)} %get-tuple-element.2) | data formatting | bytes 2097152
  41.0 0.6 %copy.13 = f32[128,128]{1,0:T(8,128)} copy(f32[128,128]{1,0:T(8,128)S(1)} %get-tuple-element.3) | data formatting | bytes 131072

commit v5 on v4

--- a/solution.py
+++ b/solution.py
@@ -58,13 +58,14 @@
         key=lambda o: (reach(o[0], tall) + reach(o[1], side), o),
     )
     mirror = [offsets.index((-dy % tall, -dx % side)) for dy, dx in offsets]
-    cuts = [0, 3 * C // 8, 3 * C // 4, C]
+    cuts = [0, 3 * C // 8, 5 * C // 8, 7 * C // 8, C]
     group = [sum(j >= cut for cut in cuts[1:]) for j in range(C)]
     return side, tall, offsets, mirror, cuts, group
 
 
 MSG, VAL, FINE, RED, HALO, COARSE = 0, 1, 2, 3, 5, 7
-TO_MSG, TO_VAL, TO_FINE, TO_RED, TO_HALO, TO_COARSE = 0, 3, 6, 7, 9, 11
+PARTS = 4
+TO_MSG, TO_VAL, TO_FINE, TO_RED, TO_HALO, TO_COARSE = 0, 4, 8, 9, 10, 12
 
 
 def kernel(
@@ -73,21 +74,13 @@
     x_out, c_out,
     amp, mask, leak, cleak, cinit, vf, vc, cnt, load_sem,
     msg_out, msg_in, val_out, val_in, fval_out, fval_in,
-    place_v, place_s, Bt, hot, dv, diag, V, rhs, W, G, side_dv, side_v,
+    place_v, place_s, Bt, hot, dv, diag, V, rhs, W, G, side_dv, side_v, side_rhs, side_diag,
     ship, land,
     red_out, red_in,
     volt1, turn, seam_out, cland,
     send_sem, recv_sem, ready,
 ):
     row, col = lax.axis_index("row"), lax.axis_index("col")
-    sources_of = (cnt_in, vc_in, vf_in, cinit_in, leak_in, cleak_in, amp_in, mask_in)
-    targets_of = (cnt, vc, vf, cinit, leak, cleak, amp, mask)
-    loads = [
-        pltpu.make_async_copy(source, target, load_sem.at[n])
-        for n, (source, target) in enumerate(zip(sources_of, targets_of))
-    ]
-    for load in loads:
-        load.start()
     TR, TC = leak.shape
     BR, BC = cleak.shape
     S = vf.shape[1]
@@ -100,12 +93,24 @@
         lax.rem(col_y + dy, tall) * side + lax.rem(col_x + dx, side) for dy, dx in offsets
     ]
 
+    sources_of = (cnt_in, vc_in, vf_in, cinit_in, leak_in, cleak_in, amp_in, mask_in)
+    targets_of = (cnt, vc, vf, cinit, leak, cleak, amp, mask)
+    loads = [
+        pltpu.make_async_copy(source, target, load_sem.at[n])
+        for n, (source, target) in enumerate(zip(sources_of, targets_of))
+    ]
+    for load in loads[:2]:
+        load.start()
+
     barrier = pltpu.get_barrier_semaphore()
-    peers = [(row, who[j]) for j in range(1, C)]
-    peers += [(lax.rem(row + d, R), col) for d in range(1, R)]
+    peers = [(lax.rem(row + d, R), col) for d in range(1, R)]
     peers += [(u, s) for u in (up, down) for s in (left, right)]
-    for peer in peers:
+    peers += [(row, who[j]) for j in range(1, C)]
+    for peer in reversed(peers):
         pl.semaphore_signal(barrier, inc=1, device_id=peer, device_id_type=pl.DeviceIdType.MESH)
+
+    for load in loads[2:]:
+        load.start()
 
     def post(src, dst, device, phase, landing):
         pltpu.make_async_remote_copy(
@@ -282,7 +287,7 @@
     hi, lo = [piece.astype(BF16) for piece in halves(cinit[...])]
     place_r = lax.broadcasted_iota(jnp.int32, (BR, per), 0)
     place_c = lax.broadcasted_iota(jnp.int32, (BC, per), 0)
-    for g in range(3):
+    for g in range(PARTS):
         arrive(span(msg_in, g), TO_MSG + g)
         for p in range(cuts[g], cuts[g + 1]):
             cut = slice(p * per, (p + 1) * per)
@@ -320,7 +325,7 @@
 
     loads[6].wait()
     loads[7].wait()
-    for g in range(3):
+    for g in range(PARTS):
         arrive(span(val_in, g), TO_VAL + g)
         cut = slice(cuts[g] * per, cuts[g + 1] * per)
         heard = jnp.concatenate([val_in[p] for p in range(cuts[g], cuts[g + 1])], axis=1)
@@ -340,7 +345,7 @@
                 else:
                     value = rhs[own(b, base, wide_step), :] + added[:, part(b)]
                 rhs[own(b, base, wide_step), :] = value
-                if g == 2:
+                if g == PARTS - 1:
                     inner = ext(0, b, base + 16, wide_step)
                     V[inner, :] = value * dv[inner, :]
             return carry
@@ -380,7 +385,7 @@
                 fresh = (fresh + fresh) - V[ext(k - 1, b, start, size), :]
             V[ext(k + 1, b, start, size), :] = fresh
 
-    core_rows = chunk_of(TR, 128)
+    core_rows = chunk_of(TR, 256)
     for k in range(ITERS - 1):
 
         def inside(i, carry, k=k):
@@ -399,85 +404,104 @@
             total = total + value[n * 8 : n * 8 + 8]
         return total
 
-    def gram(start, size, wanted, totals):
-        mid, near = near_of(ITERS - 1, start, size, wanted)
+    def products(source, low, high, v):
+        fresh = [fold(low * v[k]) for k in range(ITERS)]
+        fresh += [fold(high * v[k]) for k in range(1, ITERS)]
+        fresh += [fold(source * v[k]) for k in range(ITERS)]
+        return fresh
+
+    def gram(start, size, totals, inside):
+        mid, near = near_of(ITERS - 1, start, size, range(blocks), not inside)
         totals = list(totals)
-        for b in wanted:
+        spot = lax.broadcasted_iota(jnp.int32, (size, LANES), 1)
+        for b in range(blocks):
             at = own(b, start - 16, size)
             v = [V[ext(k, b, start, size), :] for k in range(ITERS - 1)] + [mid[b]]
             source, held = rhs[at, :], diag[at, :]
             low, high = held * (v[0] - v[1]), held * mid[b] - near[b]
-            for k in range(ITERS):
+            at_side = inside and b in (0, blocks - 1)
+            for k in range(1 if at_side else ITERS):
                 W[pl.ds((b * TR + start - 16) * ITERS + k, size, stride=ITERS), :] = v[k]
-            fresh = [fold(low * v[k]) for k in range(ITERS)]
-            fresh += [fold(high * v[k]) for k in range(1, ITERS)]
-            fresh += [fold(source * v[k]) for k in range(ITERS)]
-            totals = [x + y for x, y in zip(totals, fresh)]
+            if at_side:
+                clear = spot < 8 if b == 0 else spot >= LANES - 8
+                source, low, high = [jnp.where(clear, 0.0, part_of) for part_of in (source, low, high)]
+            totals = [x + y for x, y in zip(totals, products(source, low, high, v))]
         return tuple(totals)
 
-    tall_step = 64
+    tall_step = 128
     full = (TR - 16) // tall_step
     rest = TR - 16 - full * tall_step
 
-    def middle(wanted, totals):
-        def body(i, carry):
-            return gram(pl.multiple_of(24 + i * tall_step, 8), tall_step, wanted, carry)
-
-        totals = lax.fori_loop(0, full, body, totals)
-        if rest:
-            totals = gram(24 + full * tall_step, rest, wanted, totals)
-        return totals
-
-    totals = middle(range(1, blocks - 1), tuple(jnp.zeros((8, LANES), F32) for _ in range(sums)))
+    def interior(i, carry):
+        return gram(pl.multiple_of(24 + i * tall_step, 8), tall_step, carry, True)
+
+    totals = tuple(jnp.zeros((8, LANES), F32) for _ in range(sums))
+    totals = lax.fori_loop(0, full, interior, totals)
+    if rest:
+        totals = gram(24 + full * tall_step, rest, totals, True)
 
     rows = chunk_of(TR + 16, 176)
 
-    def low_half(size):
-        return lax.broadcasted_iota(jnp.int32, (size, LANES), 1) < LANES // 2
-
-    side_dv[8 : TR + 24, :] = jnp.where(
-        low_half(TR + 16), dv[ext(0, 0, 8, TR + 16), :], dv[ext(0, blocks - 1, 8, TR + 16), :]
-    )
+    def merge(low, high):
+        half = lax.broadcasted_iota(jnp.int32, low.shape, 1) < LANES // 2
+        return jnp.where(half, low, high)
+
+    def both_sides(F, start, size):
+        return merge(F[ext(0, 0, start, size), :], F[ext(0, blocks - 1, start, size), :])
+
+    side_dv[8 : TR + 24, :] = both_sides(dv, 8, TR + 16)
+    for held, side_of in ((rhs, side_rhs), (diag, side_diag)):
+        side_of[...] = merge(held[own(0, 0, TR), :], held[own(blocks - 1, 0, TR), :])
     halo_land(V, 1)
-    side_v[8 : TR + 24, :] = jnp.where(
-        low_half(TR + 16), V[ext(0, 0, 8, TR + 16), :], V[ext(0, blocks - 1, 8, TR + 16), :]
-    )
+    side_v[8 : TR + 24, :] = both_sides(V, 8, TR + 16)
+
+    def strip(k, start, size):
+        spot = lax.broadcasted_iota(jnp.int32, (size, LANES), 1)
+        first, last = spot == 0, spot == LANES - 1
+        inner, outer = side_v[pl.ds(k * TE + start, size), :], V[ext(k, blocks, start, size), :]
+        inner_left, inner_right = pltpu.roll(inner, 1, 1), pltpu.roll(inner, LANES - 1, 1)
+        outer_left, outer_right = pltpu.roll(outer, 1, 1), pltpu.roll(outer, LANES - 1, 1)
+        inner_near = (
+            side_v[pl.ds(k * TE + start - 1, size), :] + side_v[pl.ds(k * TE + start + 1, size), :]
+        ) + (jnp.where(first, outer_left, inner_left) + jnp.where(last, outer_right, inner_right))
+        outer_near = (
+            V[ext(k, blocks, start - 1, size), :] + V[ext(k, blocks, start + 1, size), :]
+        ) + (jnp.where(first, inner_left, outer_left) + jnp.where(last, inner_right, outer_right))
+        return inner, inner_near, outer_near
+
     for k in range(ITERS - 1):
         for start in (8, TR + 8):
             forward(k, start, 16, range(blocks))
-
-        def strips(i, carry, k=k):
-            start = pl.multiple_of(8 + i * rows, 8)
+        for start in range(8, TR + 24, rows):
+            inner_near, outer_near = strip(k, start, rows)[1:]
             spot = lax.broadcasted_iota(jnp.int32, (rows, LANES), 1)
-            first, last = spot == 0, spot == LANES - 1
-            inner, outer = side_v[pl.ds(k * TE + start, rows), :], V[ext(k, blocks, start, rows), :]
-            inner_left, inner_right = pltpu.roll(inner, 1, 1), pltpu.roll(inner, LANES - 1, 1)
-            outer_left, outer_right = pltpu.roll(outer, 1, 1), pltpu.roll(outer, LANES - 1, 1)
-            near = side_v[pl.ds(k * TE + start - 1, rows), :] + side_v[pl.ds(k * TE + start + 1, rows), :]
-            near = near + (
-                jnp.where(first, outer_left, inner_left) + jnp.where(last, outer_right, inner_right)
-            )
-            fresh = side_dv[pl.ds(start, rows), :] * near
+            fresh = side_dv[pl.ds(start, rows), :] * inner_near
             if k:
                 fresh = (fresh + fresh) - side_v[pl.ds((k - 1) * TE + start, rows), :]
             side_v[pl.ds((k + 1) * TE + start, rows), :] = fresh
             pltpu.store(V.at[ext(k + 1, 0, start, rows), :], fresh, mask=spot < 8)
             pltpu.store(V.at[ext(k + 1, blocks - 1, start, rows), :], fresh, mask=spot >= LANES - 8)
-            near = V[ext(k, blocks, start - 1, rows), :] + V[ext(k, blocks, start + 1, rows), :]
-            near = near + (
-                jnp.where(first, inner_left, outer_left) + jnp.where(last, inner_right, outer_right)
-            )
-            fresh = dv[ext(0, blocks, start, rows), :] * near
+            fresh = dv[ext(0, blocks, start, rows), :] * outer_near
             if k:
                 fresh = (fresh + fresh) - V[ext(k - 1, blocks, start, rows), :]
             V[ext(k + 1, blocks, start, rows), :] = fresh
-            return carry
-
-        lax.fori_loop(0, (TR + 16) // rows, strips, 0)
 
     for start in (16, TR + 8):
-        totals = gram(start, 8, range(blocks), totals)
-    totals = middle((0, blocks - 1), totals)
+        totals = gram(start, 8, totals, False)
+    for start in range(24, TR + 8, tall_step):
+        size = min(tall_step, TR + 8 - start)
+        inner, near = strip(ITERS - 1, start, size)[:2]
+        spot = lax.broadcasted_iota(jnp.int32, (size, LANES), 1)
+        at_edge = (spot < 8) | (spot >= LANES - 8)
+        v = [side_v[pl.ds(k * TE + start, size), :] for k in range(ITERS - 1)] + [inner]
+        for k in range(1, ITERS):
+            for b in (0, blocks - 1):
+                at = pl.ds((b * TR + start - 16) * ITERS + k, size, stride=ITERS)
+                W[at, :] = V[ext(k, b, start, size), :]
+        source, held = side_rhs[pl.ds(start - 16, size), :], side_diag[pl.ds(start - 16, size), :]
+        low, high = held * (v[0] - v[1]), held * inner - near
+        source, low, high = [jnp.where(at_edge, part_of, 0.0) for part_of in (source, low, high)]
+        totals = [x + y for x, y in zip(totals, products(source, low, high, v))]
     flat = jnp.concatenate(
         [jnp.sum(total, axis=0, keepdims=True) for total in totals]
         + [jnp.zeros((16 - sums, LANES), F32)], axis=0,
@@ -640,6 +664,7 @@
             pltpu.VMEM((ITERS * blocks * TR, LANES), F32),
             pltpu.VMEM((ITERS * S, LANES), F32),
             pltpu.VMEM((TR + 32, LANES), F32), pltpu.VMEM((ITERS * (TR + 32), LANES), F32),
+            pltpu.VMEM((TR, LANES), F32), pltpu.VMEM((TR, LANES), F32),
             pltpu.VMEM((2, 32 * blocks + 16, LANES), F32),
             pltpu.VMEM((2, 32 * blocks + 32, LANES), F32),
             pltpu.VMEM((1, LANES), F32), pltpu.VMEM((R * C, 1, LANES), F32),
@@ -647,7 +672,7 @@
             pltpu.VMEM((2, BC, BR), F32), pltpu.VMEM((2, 2, BC // GROUP, BR), F32),
             pltpu.VMEM((2, 32, BC), F32),
             pltpu.SemaphoreType.DMA((9,)),
-            pltpu.SemaphoreType.DMA((13,)),
+            pltpu.SemaphoreType.DMA((14,)),
             pltpu.SemaphoreType.REGULAR,
         ],
         compiler_params=pltpu.CompilerParams(

time: 41.7 us -> 40.4 us (0.969)
  Pallas kernels: 39.4 us -> 38 us
    pallas_call x1, Pallas kernels: 39.4 us -> 38 us  [per_device(): pl.pallas_call(functools.partial(kernel, R, C), out_shape=(pltpu.VMEM((TR...]
where the time goes in v5:
time: 40.4 us; the launch traced here: 40.3 us
  Pallas kernels  38 us (94%)
  local copies, waits for them, and re-layouts  1.6 us (4%)
  between operations  0.64 us (2%)
    pallas_call x1, Pallas kernels, per_device(): pl.pallas_call(functools.partial(kernel, R, C), out_shape=(pltpu.VMEM((TR...  38 us
    unnamed x2, local copies, waits for them, and re-layouts  1.6 us

profile of v5, /device:TPU:0, one launch (start us, length us, event | category | flops | bytes accessed | tf_op | source)
XLA Modules:
  0.0 40.3 jit_solution(1691959848054782195)
XLA Ops:
  0.6 38.0 %shard_map.95 = (f32[512,512]{1,0:T(8,128)S(1)}, f32[128,128]{1,0:T(8,128)S(1)}) custom-call(f32[512,512]{1,0:T(8,128)} %amp_in.1, s32[512,512]{1,0:T(8,128)} %mask_in.1, f32[512,512]{1,0:T(8,128)} %leak_in.1, f32[128,128]{1,0:T(8,128)} %cleak_in.1, f32[128,128]{1,0:T(8,128)} %cinit_in.1, s32[1,2048]{1,0:T(1,128)} %vf_in.1, s32[1,2048]{1,0:T(1,128)} %vc_in.1, ...), custom_call_target="tpu_custom_call" | custom-call | tf_op jit(solution)/shard_map/pallas_call | solution.py:644
  38.7 1.0 %copy.12 = f32[512,512]{1,0:T(8,128)} copy(f32[512,512]{1,0:T(8,128)S(1)} %get-tuple-element.2) | data formatting | bytes 2097152
  39.6 0.6 %copy.13 = f32[128,128]{1,0:T(8,128)} copy(f32[128,128]{1,0:T(8,128)S(1)} %get-tuple-element.3) | data formatting | bytes 131072

commit v6 on v5

--- a/solution.py
+++ b/solution.py
@@ -633,6 +633,17 @@
     c_out[...] = partial + scale * (coarse_conductance * beside(volt, 1))
 
 
+def hand_over(x_in, c_in, x_out, c_out, sem):
+    copies = [
+        pltpu.make_async_copy(x_in, x_out, sem.at[0]),
+        pltpu.make_async_copy(c_in, c_out, sem.at[1]),
+    ]
+    for copy in copies:
+        copy.start()
+    for copy in copies:
+        copy.wait()
+
+
 def per_device(R, C, load_amp, load_mask, leak, coarse_leak, coarse_init, via_fine, via_coarse, via_count):
     TR, TC = leak.shape
     BR, BC = coarse_leak.shape
@@ -641,7 +652,7 @@
     vmem = pl.BlockSpec(memory_space=pltpu.VMEM)
     blocks = TC // LANES
     ext = (blocks + 1) * (TR + 32)
-    return pl.pallas_call(
+    held = pl.pallas_call(
         functools.partial(kernel, R, C),
         out_shape=(pltpu.VMEM((TR, TC), F32), pltpu.VMEM((BR, BC), F32)),
         in_specs=[pl.BlockSpec(memory_space=pltpu.HBM)] * 8,
@@ -679,6 +690,14 @@
             collective_id=0, has_side_effects=True, vmem_limit_bytes=60 * 1024 * 1024
         ),
     )(load_amp, load_mask, leak, coarse_leak, coarse_init, via_fine, via_coarse, via_count)
+    return pl.pallas_call(
+        hand_over,
+        out_shape=(jax.ShapeDtypeStruct((TR, TC), F32), jax.ShapeDtypeStruct((BR, BC), F32)),
+        in_specs=[pl.BlockSpec(memory_space=pl.ANY)] * 2,
+        out_specs=(pl.BlockSpec(memory_space=pltpu.HBM),) * 2,
+        scratch_shapes=[pltpu.SemaphoreType.DMA((2,))],
+        compiler_params=pltpu.CompilerParams(vmem_limit_bytes=256 * 1024),
+    )(*held)
 
 
 def solution(mesh):

time: 40.4 us -> 39.8 us (0.985)
  local copies, waits for them, and re-layouts: 1.6 us -> 0 us
  Pallas kernels: 38 us -> 39 us
    unnamed x2 -> x0, local copies, waits for them, and re-layouts: 1.6 us -> none
    pallas_call x0 -> x1, Pallas kernels: none -> 0.99 us  [per_device(): pl.pallas_call(hand_over, out_shape=(jax.ShapeDtypeStruct((TR, TC), F32),...]
where the time goes in v6:
time: 39.8 us; the launch traced here: 39.7 us
  Pallas kernels  39 us (98%)
  between operations  0.64 us (2%)
    pallas_call x1, Pallas kernels, per_device(): pl.pallas_call(functools.partial(kernel, R, C), out_shape=(pltpu.VMEM((TR...  38 us
    pallas_call x1, Pallas kernels, per_device(): pl.pallas_call(hand_over, out_shape=(jax.ShapeDtypeStruct((TR, TC), F32),...  0.99 us

profile of v6, /device:TPU:0, one launch (start us, length us, event | category | flops | bytes accessed | tf_op | source)
XLA Modules:
  0.0 39.7 jit_solution(11448923787896606517)
XLA Ops:
  0.6 38.0 %shard_map.95 = (f32[512,512]{1,0:T(8,128)S(1)}, f32[128,128]{1,0:T(8,128)S(1)}) custom-call(f32[512,512]{1,0:T(8,128)} %amp_in.1, s32[512,512]{1,0:T(8,128)} %mask_in.1, f32[512,512]{1,0:T(8,128)} %leak_in.1, f32[128,128]{1,0:T(8,128)} %cleak_in.1, f32[128,128]{1,0:T(8,128)} %cinit_in.1, s32[1,2048]{1,0:T(1,128)} %vf_in.1, s32[1,2048]{1,0:T(1,128)} %vc_in.1, ...), custom_call_target="tpu_custom_call" | custom-call | tf_op jit(solution)/shard_map/pallas_call | solution.py:655
  38.7 1.0 %shard_map.96 = (f32[512,512]{1,0:T(8,128)}, f32[128,128]{1,0:T(8,128)}) custom-call(f32[512,512]{1,0:T(8,128)S(1)} %get-tuple-element.4.x_in, f32[128,128]{1,0:T(8,128)S(1)} %get-tuple-element.5.c_in), custom_call_target="tpu_custom_call" | custom-call | tf_op jit(solution)/shard_map/pallas_call | solution.py:693

commit v7 on v6

--- a/solution.py
+++ b/solution.py
@@ -65,7 +65,7 @@
 
 MSG, VAL, FINE, RED, HALO, COARSE = 0, 1, 2, 3, 5, 7
 PARTS = 4
-TO_MSG, TO_VAL, TO_FINE, TO_RED, TO_HALO, TO_COARSE = 0, 4, 8, 9, 10, 12
+TO_MSG, TO_VAL, TO_FINE, TO_RED, TO_HALO, TO_COARSE, TO_CORNER = 0, 4, 8, 9, 10, 12, 14
 
 
 def kernel(
@@ -150,13 +150,16 @@
         phase, landing = COARSE + n, TO_COARSE + n
         post(ref.at[pl.ds(0, 8)], cland.at[n, pl.ds(0, 8)], (up, col), phase, landing)
         post(ref.at[pl.ds(BR - 8, 8)], cland.at[n, pl.ds(8, 8)], (down, col), phase, landing)
+
+    def seam_send(n):
+        phase, landing = COARSE + n, TO_COARSE + n
         post(seam_out.at[n, 0], cland.at[n, pl.ds(16, 8)], (row, left), phase, landing)
         post(seam_out.at[n, 1], cland.at[n, pl.ds(24, 8)], (row, right), phase, landing)
 
     groups = BC // GROUP
 
-    def seams(volt, n):
-        turn[n] = volt.T
+    def seams(turned, n):
+        turn[n] = turned
         seam_out[n, 0] = turn[n, pl.ds(0, groups, stride=GROUP), :]
         seam_out[n, 1] = turn[n, pl.ds(GROUP - 1, groups, stride=GROUP), :]
 
@@ -182,7 +185,8 @@
         Bt[cut, :] = jnp.where(wide == lanes, 1.0, 0.0).astype(BF16)
 
     loads[3].wait()
-    seams(cinit[...], 0)
+    seams(cinit[...].T, 0)
+    seam_send(0)
     coarse_send(cinit, 0)
 
     def ext(k, b, start, size):
@@ -226,21 +230,22 @@
         sides = jnp.where(
             low_side, F[ext(0, 0, 16, TR), :], F[ext(0, blocks - 1, 16, TR), :]
         )
-        turned = sides.T
         ship[n, 4 * quad : 4 * quad + 8, :] = sides[0:8]
         ship[n, 4 * quad + 8 : 4 * quad + 16, :] = sides[TR - 8 : TR]
+        first, last = ship.at[n, pl.ds(4 * quad, 8)], ship.at[n, pl.ds(4 * quad + 8, 8)]
+        for source, q, device in (
+            (first, 3, (up, left)), (first, 2, (up, right)),
+            (last, 1, (down, left)), (last, 0, (down, right)),
+        ):
+            at = pl.ds(4 * quad + 8 * q, 8)
+            post(source, land.at[n, at], device, phase, TO_CORNER + n)
+        turned = sides.T
         for b in range(TR // LANES):
             ship[n, 2 * quad + 8 * b : 2 * quad + 8 * b + 8, :] = turned[0:8, part(b)]
             ship[n, 3 * quad + 8 * b : 3 * quad + 8 * b + 8, :] = turned[LANES - 8 : LANES, part(b)]
         for b in range(blocks):
             ship[n, 8 * b : 8 * b + 8, :] = F[ext(0, b, 16, 8), :]
             ship[n, quad + 8 * b : quad + 8 * b + 8, :] = F[ext(0, b, TR + 8, 8), :]
-        first, last = ship.at[n, pl.ds(4 * quad, 8)], ship.at[n, pl.ds(4 * quad + 8, 8)]
-        for source, q, device in (
-            (first, 3, (up, left)), (first, 2, (up, right)),
-            (last, 1, (down, left)), (last, 0, (down, right)),
-        ):
-            post(source, land.at[n, pl.ds(4 * quad + 8 * q, 8)], device, phase, landing)
         for q, device in ((2, (row, left)), (3, (row, right)), (0, (up, col)), (1, (down, col))):
             at = pl.ds(q * quad, quad)
             post(ship.at[n, at], land.at[n, at], device, phase, landing)
@@ -252,7 +257,7 @@
         return value * jnp.where(ok, 1.0, 0.0).astype(F32)
 
     def halo_land(F, n):
-        arrive(land.at[n], TO_HALO + n)
+        arrive(land.at[n, pl.ds(0, 4 * quad)], TO_HALO + n)
         for b in range(blocks):
             F[ext(0, b, 8, 8), :] = keep(top_ok, land[n, quad + 8 * b : quad + 8 * b + 8, :])
             F[ext(0, b, TR + 16, 8), :] = keep(bot_ok, land[n, 8 * b : 8 * b + 8, :])
@@ -269,6 +274,9 @@
             [keep(right_ok, low), jnp.zeros((LANES - 16, TR), F32), keep(left_ok, high)], axis=0
         )
         F[ext(0, blocks, 16, TR), :] = strip.T
+
+    def corner_land(F, n):
+        arrive(land.at[n, pl.ds(4 * quad, 32)], TO_CORNER + n)
         low8 = lax.broadcasted_iota(jnp.int32, (8, LANES), 1)
         near_low, near_high = low8 < 8, low8 >= LANES - 8
 
@@ -309,19 +317,19 @@
 
     halo_send(dv, 0)
 
-    def onto_coarse(amount):
-        spread = jnp.concatenate(
+    def spread_of(amount):
+        return jnp.concatenate(
             [
                 jnp.where(place_r == divide(msg_in[p], BC * C), amount[p], 0.0).astype(BF16)
                 for p in range(C)
             ], axis=1,
         )
-        return lax.dot_general(
-            spread, hot[...], (((1,), (1,)), ((), ())), preferred_element_type=F32
-        )
+
+    def contract(a, b):
+        return lax.dot_general(a, b, (((1,), (1,)), ((), ())), preferred_element_type=F32)
 
     loads[5].wait()
-    coarse_diag = 4.0 * coarse_conductance + cleak[...] + onto_coarse([via_conductance] * C)
+    coarse_diag = 4.0 * coarse_conductance + cleak[...] + contract(spread_of([via_conductance] * C), hot[...])
 
     loads[6].wait()
     loads[7].wait()
@@ -353,6 +361,7 @@
         lax.fori_loop(0, TR // wide_step, inject, 0)
     halo_send(V, 1)
     halo_land(dv, 0)
+    corner_land(dv, 0)
 
     def near_of(k, start, size, wanted, closed=True):
         first = lax.broadcasted_iota(jnp.int32, (size, LANES), 1) == 0
@@ -385,12 +394,13 @@
                 fresh = (fresh + fresh) - V[ext(k - 1, b, start, size), :]
             V[ext(k + 1, b, start, size), :] = fresh
 
-    core_rows = chunk_of(TR, 256)
+    core_rows, piece = chunk_of(TR, 256), 32
     for k in range(ITERS - 1):
 
         def inside(i, carry, k=k):
             start = pl.multiple_of(16 + i * core_rows, 8)
-            forward(k, start, core_rows, range(blocks), False)
+            for n in range(0, core_rows, piece):
+                forward(k, start + n, piece, range(blocks), False)
             return carry
 
         lax.fori_loop(0, TR // core_rows, inside, 0)
@@ -433,7 +443,9 @@
     rest = TR - 16 - full * tall_step
 
     def interior(i, carry):
-        return gram(pl.multiple_of(24 + i * tall_step, 8), tall_step, carry, True)
+        for n in range(0, tall_step, piece):
+            carry = gram(pl.multiple_of(24 + i * tall_step, 8) + n, piece, carry, True)
+        return carry
 
     totals = tuple(jnp.zeros((8, LANES), F32) for _ in range(sums))
     totals = lax.fori_loop(0, full, interior, totals)
@@ -469,22 +481,31 @@
         ) + (jnp.where(first, inner_left, outer_left) + jnp.where(last, inner_right, outer_right))
         return inner, inner_near, outer_near
 
-    for k in range(ITERS - 1):
+    def advance(k, start, size):
+        inner_near, outer_near = strip(k, start, size)[1:]
+        spot = lax.broadcasted_iota(jnp.int32, (size, LANES), 1)
+        fresh = side_dv[pl.ds(start, size), :] * inner_near
+        if k:
+            fresh = (fresh + fresh) - side_v[pl.ds((k - 1) * TE + start, size), :]
+        side_v[pl.ds((k + 1) * TE + start, size), :] = fresh
+        pltpu.store(V.at[ext(k + 1, 0, start, size), :], fresh, mask=spot < 8)
+        pltpu.store(V.at[ext(k + 1, blocks - 1, start, size), :], fresh, mask=spot >= LANES - 8)
+        fresh = dv[ext(0, blocks, start, size), :] * outer_near
+        if k:
+            fresh = (fresh + fresh) - V[ext(k - 1, blocks, start, size), :]
+        V[ext(k + 1, blocks, start, size), :] = fresh
+
+    for start in range(24, TR + 8, rows):
+        advance(0, start, min(rows, TR + 8 - start))
+    corner_land(V, 1)
+    for start in (8, TR + 8):
+        advance(0, start, 16)
+        forward(0, start, 16, range(blocks))
+    for k in range(1, ITERS - 1):
         for start in (8, TR + 8):
             forward(k, start, 16, range(blocks))
         for start in range(8, TR + 24, rows):
-            inner_near, outer_near = strip(k, start, rows)[1:]
-            spot = lax.broadcasted_iota(jnp.int32, (rows, LANES), 1)
-            fresh = side_dv[pl.ds(start, rows), :] * inner_near
-            if k:
-                fresh = (fresh + fresh) - side_v[pl.ds((k - 1) * TE + start, rows), :]
-            side_v[pl.ds((k + 1) * TE + start, rows), :] = fresh
-            pltpu.store(V.at[ext(k + 1, 0, start, rows), :], fresh, mask=spot < 8)
-            pltpu.store(V.at[ext(k + 1, blocks - 1, start, rows), :], fresh, mask=spot >= LANES - 8)
-            fresh = dv[ext(0, blocks, start, rows), :] * outer_near
-            if k:
-                fresh = (fresh + fresh) - V[ext(k - 1, blocks, start, rows), :]
-            V[ext(k + 1, blocks, start, rows), :] = fresh
+            advance(k, start, rows)
 
     for start in (16, TR + 8):
         totals = gram(start, 8, totals, False)
@@ -513,12 +534,19 @@
     red_out[...] = jnp.sum(jnp.where(same, number, 0.0), axis=0, keepdims=True)
     red_in[0] = red_out[...]
     pl.semaphore_wait(ready, R - 1)
-    for d in sorted(range(R), key=lambda d: -min(d, R - d)):
-        for j in reversed(range(C)):
-            if d or j:
+    hops = {
+        (d, j): (min(d, R - d) + 1) // 2 + min(dy, tall - dy) + min(dx, side - dx)
+        for d in range(R) for j, (dy, dx) in enumerate(offsets) if d or j
+    }
+    order = sorted(hops, key=lambda at: -hops[at])
+
+    def tell(near):
+        for d, j in order:
+            if (hops[d, j] < 4) == near:
                 slot = (R - d) % R * C + mirror[j]
                 post(red_out, red_in.at[slot], (lax.rem(row + d, R), who[j]), RED, TO_RED)
 
+    tell(False)
     move.wait()
     reach = 64
     turned_lane = lax.broadcasted_iota(jnp.int32, (LANES, per), 0)
@@ -542,6 +570,8 @@
                 )
         for j in reversed(range(max(first, 1), first + flock)):
             post(fval_out.at[j], fval_in.at[mirror[j]], (row, who[j]), FINE, TO_FINE)
+        if first + flock == C:
+            tell(True)
     fval_in[0] = fval_out[0]
 
     place = lax.broadcasted_iota(jnp.int32, (BR, BC), 1)
@@ -571,9 +601,16 @@
     volt = cinit[...]
     scale = relaxation / coarse_diag
     partial = volt + scale * (coarse_conductance * beside(volt, 0) - coarse_diag * volt)
+    partial_turned, scale_turned = partial.T, scale.T
 
     arrive(red_in.at[pl.ds(1, R * C - 1)], TO_RED)
-    total = jnp.sum(red_in[...], axis=0)
+    heard = [red_in[pl.ds(j * R, R)] for j in range(C)]
+    while len(heard) > 1:
+        heard = [a + b for a, b in zip(heard[::2], heard[1::2])]
+    total = heard[0]
+    while total.shape[0] > 1:
+        total = total[: total.shape[0] // 2] + total[total.shape[0] // 2 :]
+    total = total[0]
     number = jnp.sum(jnp.where(same, jnp.broadcast_to(total, (16, LANES)), 0.0), axis=1, keepdims=True)
     number = [number[n : n + 1, :] for n in range(sums)]
 
@@ -604,10 +641,15 @@
         for k in range(1, ITERS):
             found = found + coef[k] * fval_in[p, k : k + 1, :]
         amount.append(halves(via_conductance * found))
-    sources = onto_coarse([a[0] for a in amount]) + onto_coarse([a[1] for a in amount])
+    spread = jnp.concatenate([spread_of(piece_of) for piece_of in zip(*amount)], axis=0)
+    found = contract(hot[...], spread)
+    found = found[:, :BR] + found[:, BR:]
+    cross = partial_turned + scale_turned * found
+    seams(cross, 1)
+    seam_send(1)
+    sources = found.T
     volt = partial + scale * sources
     volt1[...] = volt
-    seams(volt, 1)
     coarse_send(volt1, 1)
     partial = volt + scale * (sources - coarse_diag * volt)
     step = 64
@@ -634,10 +676,12 @@
 
 
 def hand_over(x_in, c_in, x_out, c_out, sem):
+    step = x_in.shape[0] // 4
     copies = [
-        pltpu.make_async_copy(x_in, x_out, sem.at[0]),
-        pltpu.make_async_copy(c_in, c_out, sem.at[1]),
+        pltpu.make_async_copy(x_in.at[pl.ds(n * step, step)], x_out.at[pl.ds(n * step, step)], sem.at[n])
+        for n in range(4)
     ]
+    copies.append(pltpu.make_async_copy(c_in, c_out, sem.at[4]))
     for copy in copies:
         copy.start()
     for copy in copies:
@@ -683,7 +727,7 @@
             pltpu.VMEM((2, BC, BR), F32), pltpu.VMEM((2, 2, BC // GROUP, BR), F32),
             pltpu.VMEM((2, 32, BC), F32),
             pltpu.SemaphoreType.DMA((9,)),
-            pltpu.SemaphoreType.DMA((14,)),
+            pltpu.SemaphoreType.DMA((16,)),
             pltpu.SemaphoreType.REGULAR,
         ],
         compiler_params=pltpu.CompilerParams(
@@ -695,7 +739,7 @@
         out_shape=(jax.ShapeDtypeStruct((TR, TC), F32), jax.ShapeDtypeStruct((BR, BC), F32)),
         in_specs=[pl.BlockSpec(memory_space=pl.ANY)] * 2,
         out_specs=(pl.BlockSpec(memory_space=pltpu.HBM),) * 2,
-        scratch_shapes=[pltpu.SemaphoreType.DMA((2,))],
+        scratch_shapes=[pltpu.SemaphoreType.DMA((5,))],
         compiler_params=pltpu.CompilerParams(vmem_limit_bytes=256 * 1024),
     )(*held)
 

time: 39.8 us -> 39.2 us (0.985)
  Pallas kernels: 39 us -> 38.5 us
    pallas_call x1, Pallas kernels: 38 us -> 37.4 us  [per_device(): pl.pallas_call(functools.partial(kernel, R, C), out_shape=(pltpu.VMEM((TR...]
where the time goes in v7:
time: 39.2 us; the launch traced here: 39.1 us
  Pallas kernels  38.5 us (98%)
  between operations  0.64 us (2%)
    pallas_call x1, Pallas kernels, per_device(): pl.pallas_call(functools.partial(kernel, R, C), out_shape=(pltpu.VMEM((TR...  37.4 us
    pallas_call x1, Pallas kernels, per_device(): pl.pallas_call(hand_over, out_shape=(jax.ShapeDtypeStruct((TR, TC), F32),...  1.02 us

profile of v7, /device:TPU:0, one launch (start us, length us, event | category | flops | bytes accessed | tf_op | source)
XLA Modules:
  0.0 39.1 jit_solution(13723715678822484868)
XLA Ops:
  0.6 37.4 %shard_map.95 = (f32[512,512]{1,0:T(8,128)S(1)}, f32[128,128]{1,0:T(8,128)S(1)}) custom-call(f32[512,512]{1,0:T(8,128)} %amp_in.1, s32[512,512]{1,0:T(8,128)} %mask_in.1, f32[512,512]{1,0:T(8,128)} %leak_in.1, f32[128,128]{1,0:T(8,128)} %cleak_in.1, f32[128,128]{1,0:T(8,128)} %cinit_in.1, s32[1,2048]{1,0:T(1,128)} %vf_in.1, s32[1,2048]{1,0:T(1,128)} %vc_in.1, ...), custom_call_target="tpu_custom_call" | custom-call | tf_op jit(solution)/shard_map/pallas_call | solution.py:699
  38.1 1.0 %shard_map.96 = (f32[512,512]{1,0:T(8,128)}, f32[128,128]{1,0:T(8,128)}) custom-call(f32[512,512]{1,0:T(8,128)S(1)} %get-tuple-element.4.x_in, f32[128,128]{1,0:T(8,128)S(1)} %get-tuple-element.5.c_in), custom_call_target="tpu_custom_call" | custom-call | tf_op jit(solution)/shard_map/pallas_call | solution.py:737

commit v8 on v7

--- a/solution.py
+++ b/solution.py
@@ -74,7 +74,7 @@
     x_out, c_out,
     amp, mask, leak, cleak, cinit, vf, vc, cnt, load_sem,
     msg_out, msg_in, val_out, val_in, fval_out, fval_in,
-    place_v, place_s, Bt, hot, dv, diag, V, rhs, W, G, side_dv, side_v, side_rhs, side_diag,
+    place_v, place_s, Bt, hot, dv, diag, V, rhs, W, G, side_v, turn_dv, turn_v, turn_rhs, turn_diag,
     ship, land,
     red_out, red_in,
     volt1, turn, seam_out, cland,
@@ -173,7 +173,8 @@
     fine_col = remainder(fine, TC)
     TE = TR + 32
     blocks = TC // LANES
-    all_blocks = blocks + 1
+    ring = blocks + 1
+    TURN = 48
     place_v[...] = (divide(fine_col, LANES) * TR + fine_row) * ITERS
     move = pltpu.make_async_copy(place_v, place_s, load_sem.at[8])
     move.start()
@@ -190,7 +191,10 @@
     coarse_send(cinit, 0)
 
     def ext(k, b, start, size):
-        return pl.ds((k * all_blocks + b) * TE + start, size)
+        return pl.ds((k * blocks + b) * TE + start, size)
+
+    def pt(k, b, start, size):
+        return pl.ds((k * ring + b) * TURN + start, size)
 
     def own(b, start, size):
         return pl.ds(b * TR + start, size)
@@ -200,11 +204,12 @@
 
     zero_pad = jnp.zeros((8, LANES), F32)
     for n in range(ITERS):
-        for b in range(all_blocks):
+        for b in range(blocks):
             V[ext(n, b, 0, 8), :] = zero_pad
             V[ext(n, b, TR + 24, 8), :] = zero_pad
-        side_v[pl.ds(n * TE, 8), :] = zero_pad
-        side_v[pl.ds(n * TE + TR + 24, 8), :] = zero_pad
+        for b in range(ring):
+            turn_v[pt(n, b, 0, 8), :] = zero_pad
+            turn_v[pt(n, b, TURN - 8, 8), :] = zero_pad
 
     loads[4].wait()
     wide_step = 256 if TR % 256 == 0 else 64
@@ -256,26 +261,34 @@
     def keep(ok, value):
         return value * jnp.where(ok, 1.0, 0.0).astype(F32)
 
-    def halo_land(F, n):
+    def stand(low, high):
+        tall = jnp.concatenate([low, jnp.zeros((LANES - 16, low.shape[1]), F32), high], axis=0)
+        return tall.T
+
+    def merge(low, high):
+        half = lax.broadcasted_iota(jnp.int32, low.shape, 1) < LANES // 2
+        return jnp.where(half, low, high)
+
+    def halo_land(F, n, turned):
         arrive(land.at[n, pl.ds(0, 4 * quad)], TO_HALO + n)
+        above = [
+            keep(top_ok, land[n, quad + 8 * b : quad + 8 * b + 8, :]) for b in range(blocks)
+        ]
+        below = [keep(bot_ok, land[n, 8 * b : 8 * b + 8, :]) for b in range(blocks)]
         for b in range(blocks):
-            F[ext(0, b, 8, 8), :] = keep(top_ok, land[n, quad + 8 * b : quad + 8 * b + 8, :])
-            F[ext(0, b, TR + 16, 8), :] = keep(bot_ok, land[n, 8 * b : 8 * b + 8, :])
-        low, high = [
-            jnp.concatenate(
-                [
-                    land[n, q * quad + 8 * b : q * quad + 8 * b + 8, :]
-                    for b in range(TR // LANES)
-                ], axis=1,
-            )
-            for q in (2, 3)
-        ]
-        strip = jnp.concatenate(
-            [keep(right_ok, low), jnp.zeros((LANES - 16, TR), F32), keep(left_ok, high)], axis=0
-        )
-        F[ext(0, blocks, 16, TR), :] = strip.T
-
-    def corner_land(F, n):
+            F[ext(0, b, 8, 8), :] = above[b]
+            F[ext(0, b, TR + 16, 8), :] = below[b]
+        for b in range(TR // LANES):
+            at_low, at_high = 2 * quad + 8 * b, 3 * quad + 8 * b
+            turned[pt(0, b, 8, 8), :] = keep(left_ok, land[n, at_high : at_high + 8, :])
+            turned[pt(0, b, 16, 8), :] = ship[n, at_low : at_low + 8, :]
+            turned[pt(0, b, 24, 8), :] = ship[n, at_high : at_high + 8, :]
+            turned[pt(0, b, 32, 8), :] = keep(right_ok, land[n, at_low : at_low + 8, :])
+        ends = stand(merge(below[0], below[-1]), merge(above[0], above[-1]))
+        turned[pt(0, blocks, 16, 8), :] = ends[0:8]
+        turned[pt(0, blocks, 24, 8), :] = ends[LANES - 8 : LANES]
+
+    def corner_land(n, turned):
         arrive(land.at[n, pl.ds(4 * quad, 32)], TO_CORNER + n)
         low8 = lax.broadcasted_iota(jnp.int32, (8, LANES), 1)
         near_low, near_high = low8 < 8, low8 >= LANES - 8
@@ -289,8 +302,9 @@
                 + jnp.where(near_high, keep(left_ok, hi), 0.0),
             )
 
-        F[ext(0, blocks, 8, 8), :] = corner(top_ok, 1, 0)
-        F[ext(0, blocks, TR + 16, 8), :] = corner(bot_ok, 3, 2)
+        ends = stand(corner(bot_ok, 3, 2), corner(top_ok, 1, 0))
+        turned[pt(0, blocks, 32, 8), :] = ends[0:8]
+        turned[pt(0, blocks, 8, 8), :] = ends[LANES - 8 : LANES]
 
     hi, lo = [piece.astype(BF16) for piece in halves(cinit[...])]
     place_r = lax.broadcasted_iota(jnp.int32, (BR, per), 0)
@@ -360,47 +374,60 @@
 
         lax.fori_loop(0, TR // wide_step, inject, 0)
     halo_send(V, 1)
-    halo_land(dv, 0)
-    corner_land(dv, 0)
-
-    def near_of(k, start, size, wanted, closed=True):
+    halo_land(dv, 0, turn_dv)
+    corner_land(0, turn_dv)
+
+    def lean(mid):
+        size, count = mid[0].shape[0], len(mid)
         first = lax.broadcasted_iota(jnp.int32, (size, LANES), 1) == 0
         last = lax.broadcasted_iota(jnp.int32, (size, LANES), 1) == LANES - 1
-        mid, before, after = {}, {}, {}
-        for b in wanted:
-            for near in (b - 1, b, b + 1):
-                near = near % all_blocks
-                if near not in mid and (closed or near < blocks):
-                    mid[near] = V[ext(k, near, start, size), :]
-        for b in mid:
-            before[b] = pltpu.roll(mid[b], 1, 1)
-            after[b] = pltpu.roll(mid[b], LANES - 1, 1)
-        found = {}
-        for b in wanted:
-            tall = V[ext(k, b, start - 1, size), :] + V[ext(k, b, start + 1, size), :]
-            left_of, right_of = before[b], after[b]
-            if closed or b:
-                left_of = jnp.where(first, before[(b - 1) % all_blocks], left_of)
-            if closed or b < blocks - 1:
-                right_of = jnp.where(last, after[(b + 1) % all_blocks], right_of)
-            found[b] = tall + (left_of + right_of)
+        before = [pltpu.roll(m, 1, 1) for m in mid]
+        after = [pltpu.roll(m, LANES - 1, 1) for m in mid]
+        return [
+            jnp.where(first, before[b - 1], before[b])
+            + jnp.where(last, after[(b + 1) % count], after[b])
+            for b in range(count)
+        ]
+
+    def near_of(k, start, size):
+        mid = [V[ext(k, b, start, size), :] for b in range(blocks)]
+        found = [
+            V[ext(k, b, start - 1, size), :] + V[ext(k, b, start + 1, size), :] + across
+            for b, across in enumerate(lean(mid))
+        ]
         return mid, found
 
-    def forward(k, start, size, wanted, closed=True):
-        near = near_of(k, start, size, wanted, closed)[1]
-        for b in wanted:
+    def forward(k, start, size):
+        near = near_of(k, start, size)[1]
+        for b in range(blocks):
             fresh = dv[ext(0, b, start, size), :] * near[b]
             if k:
                 fresh = (fresh + fresh) - V[ext(k - 1, b, start, size), :]
             V[ext(k + 1, b, start, size), :] = fresh
 
+    def turned_near(k):
+        mid = [turn_v[pt(k, b, 8, 32), :] for b in range(ring)]
+        found = [
+            turn_v[pt(k, b, 7, 32), :] + turn_v[pt(k, b, 9, 32), :] + across
+            for b, across in enumerate(lean(mid))
+        ]
+        return mid, found
+
+    def turned_forward(k):
+        near = turned_near(k)[1]
+        for b in range(ring):
+            fresh = turn_dv[pt(0, b, 8, 32), :] * near[b]
+            if k:
+                fresh = (fresh + fresh) - turn_v[pt(k - 1, b, 8, 32), :]
+            turn_v[pt(k + 1, b, 8, 32), :] = fresh
+
     core_rows, piece = chunk_of(TR, 256), 32
     for k in range(ITERS - 1):
 
         def inside(i, carry, k=k):
             start = pl.multiple_of(16 + i * core_rows, 8)
             for n in range(0, core_rows, piece):
-                forward(k, start + n, piece, range(blocks), False)
+                forward(k, start + n, piece)
             return carry
 
         lax.fori_loop(0, TR // core_rows, inside, 0)
@@ -420,8 +447,8 @@
         fresh += [fold(source * v[k]) for k in range(ITERS)]
         return fresh
 
-    def gram(start, size, totals, inside):
-        mid, near = near_of(ITERS - 1, start, size, range(blocks), not inside)
+    def gram(start, size, totals):
+        mid, near = near_of(ITERS - 1, start, size)
         totals = list(totals)
         spot = lax.broadcasted_iota(jnp.int32, (size, LANES), 1)
         for b in range(blocks):
@@ -429,11 +456,11 @@
             v = [V[ext(k, b, start, size), :] for k in range(ITERS - 1)] + [mid[b]]
             source, held = rhs[at, :], diag[at, :]
             low, high = held * (v[0] - v[1]), held * mid[b] - near[b]
-            at_side = inside and b in (0, blocks - 1)
+            at_side = b in (0, blocks - 1)
             for k in range(1 if at_side else ITERS):
                 W[pl.ds((b * TR + start - 16) * ITERS + k, size, stride=ITERS), :] = v[k]
             if at_side:
-                clear = spot < 8 if b == 0 else spot >= LANES - 8
+                clear = spot < 4 if b == 0 else spot >= LANES - 4
                 source, low, high = [jnp.where(clear, 0.0, part_of) for part_of in (source, low, high)]
             totals = [x + y for x, y in zip(totals, products(source, low, high, v))]
         return tuple(totals)
@@ -444,85 +471,41 @@
 
     def interior(i, carry):
         for n in range(0, tall_step, piece):
-            carry = gram(pl.multiple_of(24 + i * tall_step, 8) + n, piece, carry, True)
+            carry = gram(pl.multiple_of(24 + i * tall_step, 8) + n, piece, carry)
         return carry
 
     totals = tuple(jnp.zeros((8, LANES), F32) for _ in range(sums))
     totals = lax.fori_loop(0, full, interior, totals)
     if rest:
-        totals = gram(24 + full * tall_step, rest, totals, True)
-
-    rows = chunk_of(TR + 16, 176)
-
-    def merge(low, high):
-        half = lax.broadcasted_iota(jnp.int32, low.shape, 1) < LANES // 2
-        return jnp.where(half, low, high)
-
-    def both_sides(F, start, size):
-        return merge(F[ext(0, 0, start, size), :], F[ext(0, blocks - 1, start, size), :])
-
-    side_dv[8 : TR + 24, :] = both_sides(dv, 8, TR + 16)
-    for held, side_of in ((rhs, side_rhs), (diag, side_diag)):
-        side_of[...] = merge(held[own(0, 0, TR), :], held[own(blocks - 1, 0, TR), :])
-    halo_land(V, 1)
-    side_v[8 : TR + 24, :] = both_sides(V, 8, TR + 16)
-
-    def strip(k, start, size):
-        spot = lax.broadcasted_iota(jnp.int32, (size, LANES), 1)
-        first, last = spot == 0, spot == LANES - 1
-        inner, outer = side_v[pl.ds(k * TE + start, size), :], V[ext(k, blocks, start, size), :]
-        inner_left, inner_right = pltpu.roll(inner, 1, 1), pltpu.roll(inner, LANES - 1, 1)
-        outer_left, outer_right = pltpu.roll(outer, 1, 1), pltpu.roll(outer, LANES - 1, 1)
-        inner_near = (
-            side_v[pl.ds(k * TE + start - 1, size), :] + side_v[pl.ds(k * TE + start + 1, size), :]
-        ) + (jnp.where(first, outer_left, inner_left) + jnp.where(last, outer_right, inner_right))
-        outer_near = (
-            V[ext(k, blocks, start - 1, size), :] + V[ext(k, blocks, start + 1, size), :]
-        ) + (jnp.where(first, inner_left, outer_left) + jnp.where(last, inner_right, outer_right))
-        return inner, inner_near, outer_near
-
-    def advance(k, start, size):
-        inner_near, outer_near = strip(k, start, size)[1:]
-        spot = lax.broadcasted_iota(jnp.int32, (size, LANES), 1)
-        fresh = side_dv[pl.ds(start, size), :] * inner_near
-        if k:
-            fresh = (fresh + fresh) - side_v[pl.ds((k - 1) * TE + start, size), :]
-        side_v[pl.ds((k + 1) * TE + start, size), :] = fresh
-        pltpu.store(V.at[ext(k + 1, 0, start, size), :], fresh, mask=spot < 8)
-        pltpu.store(V.at[ext(k + 1, blocks - 1, start, size), :], fresh, mask=spot >= LANES - 8)
-        fresh = dv[ext(0, blocks, start, size), :] * outer_near
-        if k:
-            fresh = (fresh + fresh) - V[ext(k - 1, blocks, start, size), :]
-        V[ext(k + 1, blocks, start, size), :] = fresh
-
-    for start in range(24, TR + 8, rows):
-        advance(0, start, min(rows, TR + 8 - start))
-    corner_land(V, 1)
+        totals = gram(24 + full * tall_step, rest, totals)
+
+    for held, turned_of in ((rhs, turn_rhs), (diag, turn_diag)):
+        turned = merge(held[own(0, 0, TR), :], held[own(blocks - 1, 0, TR), :]).T
+        for b in range(TR // LANES):
+            turned_of[pl.ds(16 * b, 8), :] = turned[0:8, part(b)]
+            turned_of[pl.ds(16 * b + 8, 8), :] = turned[LANES - 8 : LANES, part(b)]
+
+    halo_land(V, 1, turn_v)
     for start in (8, TR + 8):
-        advance(0, start, 16)
-        forward(0, start, 16, range(blocks))
+        forward(0, start, 16)
+    corner_land(1, turn_v)
+    turned_forward(0)
     for k in range(1, ITERS - 1):
         for start in (8, TR + 8):
-            forward(k, start, 16, range(blocks))
-        for start in range(8, TR + 24, rows):
-            advance(k, start, rows)
-
+            forward(k, start, 16)
+        turned_forward(k)
     for start in (16, TR + 8):
-        totals = gram(start, 8, totals, False)
-    for start in range(24, TR + 8, tall_step):
-        size = min(tall_step, TR + 8 - start)
-        inner, near = strip(ITERS - 1, start, size)[:2]
-        spot = lax.broadcasted_iota(jnp.int32, (size, LANES), 1)
-        at_edge = (spot < 8) | (spot >= LANES - 8)
-        v = [side_v[pl.ds(k * TE + start, size), :] for k in range(ITERS - 1)] + [inner]
-        for k in range(1, ITERS):
-            for b in (0, blocks - 1):
-                at = pl.ds((b * TR + start - 16) * ITERS + k, size, stride=ITERS)
-                W[at, :] = V[ext(k, b, start, size), :]
-        source, held = side_rhs[pl.ds(start - 16, size), :], side_diag[pl.ds(start - 16, size), :]
-        low, high = held * (v[0] - v[1]), held * inner - near
-        source, low, high = [jnp.where(at_edge, part_of, 0.0) for part_of in (source, low, high)]
+        totals = gram(start, 8, totals)
+    mid, near = turned_near(ITERS - 1)
+    depth = lax.broadcasted_iota(jnp.int32, (16, LANES), 0)
+    outer = (depth < 4) | (depth >= 12)
+    for b in range(TR // LANES):
+        v = [turn_v[pt(k, b, 16, 16), :] for k in range(ITERS - 1)] + [mid[b][8:24]]
+        source, held = turn_rhs[pl.ds(16 * b, 16), :], turn_diag[pl.ds(16 * b, 16), :]
+        low, high = held * (v[0] - v[1]), held * v[ITERS - 1] - near[b][8:24]
+        source, low, high = [jnp.where(outer, part_of, 0.0) for part_of in (source, low, high)]
         totals = [x + y for x, y in zip(totals, products(source, low, high, v))]
+
     flat = jnp.concatenate(
         [jnp.sum(total, axis=0, keepdims=True) for total in totals]
         + [jnp.zeros((16 - sums, LANES), F32)], axis=0,
@@ -547,6 +530,18 @@
                 post(red_out, red_in.at[slot], (lax.rem(row + d, R), who[j]), RED, TO_RED)
 
     tell(False)
+    spot = lax.broadcasted_iota(jnp.int32, (TR, LANES), 1)
+    edges = ((0, spot < 4), (blocks - 1, spot >= LANES - 4))
+    for k in range(1, ITERS):
+        low, high = [
+            jnp.concatenate([turn_v[pt(k, b, at, 8), :] for b in range(TR // LANES)], axis=1)
+            for at in (16, 24)
+        ]
+        side = stand(low, high)
+        side_v[pl.ds((k - 1) * TR, TR), :] = side
+        for b, mask_of in edges:
+            at = pl.ds(b * TR * ITERS + k, TR, stride=ITERS)
+            W[at, :] = jnp.where(mask_of, side, V[ext(k, b, 16, TR), :])
     move.wait()
     reach = 64
     turned_lane = lax.broadcasted_iota(jnp.int32, (LANES, per), 0)
@@ -596,6 +591,11 @@
         before = jnp.where(within == 0, edge, pltpu.roll(volt, 1, 1))
         after = jnp.where(within == GROUP - 1, edge, pltpu.roll(volt, BC - 1, 1))
         return above + below + before + after
+
+    for k in range(1, ITERS):
+        for b, mask_of in edges:
+            held = side_v[pl.ds((k - 1) * TR, TR), :]
+            pltpu.store(V.at[ext(k, b, 16, TR), :], held, mask=mask_of)
 
     arrive(cland.at[0], TO_COARSE)
     volt = cinit[...]
@@ -695,7 +695,7 @@
     per = S // C
     vmem = pl.BlockSpec(memory_space=pltpu.VMEM)
     blocks = TC // LANES
-    ext = (blocks + 1) * (TR + 32)
+    ext = blocks * (TR + 32)
     held = pl.pallas_call(
         functools.partial(kernel, R, C),
         out_shape=(pltpu.VMEM((TR, TC), F32), pltpu.VMEM((BR, BC), F32)),
@@ -718,8 +718,10 @@
             pltpu.VMEM((blocks * TR, LANES), F32),
             pltpu.VMEM((ITERS * blocks * TR, LANES), F32),
             pltpu.VMEM((ITERS * S, LANES), F32),
-            pltpu.VMEM((TR + 32, LANES), F32), pltpu.VMEM((ITERS * (TR + 32), LANES), F32),
-            pltpu.VMEM((TR, LANES), F32), pltpu.VMEM((TR, LANES), F32),
+            pltpu.VMEM(((ITERS - 1) * TR, LANES), F32),
+            pltpu.VMEM(((blocks + 1) * 48, LANES), F32),
+            pltpu.VMEM((ITERS * (blocks + 1) * 48, LANES), F32),
+            pltpu.VMEM((TR // 8, LANES), F32), pltpu.VMEM((TR // 8, LANES), F32),
             pltpu.VMEM((2, 32 * blocks + 16, LANES), F32),
             pltpu.VMEM((2, 32 * blocks + 32, LANES), F32),
             pltpu.VMEM((1, LANES), F32), pltpu.VMEM((R * C, 1, LANES), F32),

time: 39.2 us -> 38.4 us (0.980)
  Pallas kernels: 38.5 us -> 37.6 us
    pallas_call x1, Pallas kernels: 37.4 us -> 36.6 us  [per_device(): pl.pallas_call(functools.partial(kernel, R, C), out_shape=(pltpu.VMEM((TR...]
where the time goes in v8:
time: 38.4 us; the launch traced here: 38.3 us
  Pallas kernels  37.6 us (98%)
  between operations  0.64 us (2%)
    pallas_call x1, Pallas kernels, per_device(): pl.pallas_call(functools.partial(kernel, R, C), out_shape=(pltpu.VMEM((TR...  36.6 us
    pallas_call x1, Pallas kernels, per_device(): pl.pallas_call(hand_over, out_shape=(jax.ShapeDtypeStruct((TR, TC), F32),...  1.02 us

profile of v8, /device:TPU:0, one launch (start us, length us, event | category | flops | bytes accessed | tf_op | source)
XLA Modules:
  0.0 38.3 jit_solution(11781084886623615949)
XLA Ops:
  0.6 36.6 %shard_map.95 = (f32[512,512]{1,0:T(8,128)S(1)}, f32[128,128]{1,0:T(8,128)S(1)}) custom-call(f32[512,512]{1,0:T(8,128)} %amp_in.1, s32[512,512]{1,0:T(8,128)} %mask_in.1, f32[512,512]{1,0:T(8,128)} %leak_in.1, f32[128,128]{1,0:T(8,128)} %cleak_in.1, f32[128,128]{1,0:T(8,128)} %cinit_in.1, s32[1,2048]{1,0:T(1,128)} %vf_in.1, s32[1,2048]{1,0:T(1,128)} %vc_in.1, ...), custom_call_target="tpu_custom_call" | custom-call | tf_op jit(solution)/shard_map/pallas_call | solution.py:699
  37.2 1.0 %shard_map.96 = (f32[512,512]{1,0:T(8,128)}, f32[128,128]{1,0:T(8,128)}) custom-call(f32[512,512]{1,0:T(8,128)S(1)} %get-tuple-element.4.x_in, f32[128,128]{1,0:T(8,128)S(1)} %get-tuple-element.5.c_in), custom_call_target="tpu_custom_call" | custom-call | tf_op jit(solution)/shard_map/pallas_call | solution.py:739

commit v9 on v8

--- a/solution.py
+++ b/solution.py
@@ -74,7 +74,7 @@
     x_out, c_out,
     amp, mask, leak, cleak, cinit, vf, vc, cnt, load_sem,
     msg_out, msg_in, val_out, val_in, fval_out, fval_in,
-    place_v, place_s, Bt, hot, dv, diag, V, rhs, W, G, side_v, turn_dv, turn_v, turn_rhs, turn_diag,
+    place_v, place_s, Bt, hot, dv, diag, V, rhs, W, G0, G1, lane_of, side_v, turn_dv, turn_v, turn_rhs, turn_diag,
     ship, land,
     red_out, red_in,
     volt1, turn, seam_out, cland,
@@ -176,6 +176,8 @@
     ring = blocks + 1
     TURN = 48
     place_v[...] = (divide(fine_col, LANES) * TR + fine_row) * ITERS
+    for j in range(C):
+        lane_of[j] = remainder(fine_col, LANES)[:, j * per : (j + 1) * per]
     move = pltpu.make_async_copy(place_v, place_s, load_sem.at[8])
     move.start()
     lanes = lax.broadcasted_iota(jnp.int32, (per, TC), 1).astype(F32)
@@ -523,13 +525,13 @@
     }
     order = sorted(hops, key=lambda at: -hops[at])
 
-    def tell(near):
+    def tell(least, most):
         for d, j in order:
-            if (hops[d, j] < 4) == near:
+            if least <= hops[d, j] <= most:
                 slot = (R - d) % R * C + mirror[j]
                 post(red_out, red_in.at[slot], (lax.rem(row + d, R), who[j]), RED, TO_RED)
 
-    tell(False)
+    tell(4, R * C)
     spot = lax.broadcasted_iota(jnp.int32, (TR, LANES), 1)
     edges = ((0, spot < 4), (blocks - 1, spot >= LANES - 4))
     for k in range(1, ITERS):
@@ -543,30 +545,34 @@
             at = pl.ds(b * TR * ITERS + k, TR, stride=ITERS)
             W[at, :] = jnp.where(mask_of, side, V[ext(k, b, 16, TR), :])
     move.wait()
-    reach = 64
     turned_lane = lax.broadcasted_iota(jnp.int32, (LANES, per), 0)
-    fine_lane = remainder(fine_col, LANES)
     flock = max(C // 4, 1)
-    for first in reversed(range(0, C, flock)):
-
-        def fetch(i, carry, first=first):
-            for j in range(reach):
-                s = first * per + i * reach + j
-                G[pl.ds(s * ITERS, ITERS), :] = W[pl.ds(place_s[0, s], ITERS), :]
+    firsts = list(reversed(range(0, C, flock)))
+    for turn_of in range(len(firsts) + 1):
+        ahead = firsts[turn_of] if turn_of < len(firsts) else None
+        behind = firsts[turn_of - 1] if turn_of else None
+        into, out_of = (G0, G1) if turn_of % 2 else (G1, G0)
+
+        def fetch_turn(i, carry, ahead=ahead, behind=behind, into=into, out_of=out_of):
+            if behind is not None:
+                pick = turned_lane == lane_of[behind + i]
+                for k in range(ITERS):
+                    turned = out_of[pl.ds(i * per * ITERS + k, per, stride=ITERS), :].T
+                    fval_out[behind + i, k : k + 1, :] = jnp.sum(
+                        jnp.where(pick, turned, 0.0), axis=0, keepdims=True
+                    )
+            if ahead is not None:
+                for j in range(per):
+                    at = place_s[0, (ahead + i) * per + j]
+                    into[pl.ds((i * per + j) * ITERS, ITERS), :] = W[pl.ds(at, ITERS), :]
             return carry
 
-        lax.fori_loop(0, flock * per // reach, fetch, 0)
-        for j in reversed(range(first, first + flock)):
-            pick = turned_lane == fine_lane[:, j * per : (j + 1) * per]
-            for k in range(ITERS):
-                turned = G[pl.ds(j * per * ITERS + k, per, stride=ITERS), :].T
-                fval_out[j, k : k + 1, :] = jnp.sum(
-                    jnp.where(pick, turned, 0.0), axis=0, keepdims=True
-                )
-        for j in reversed(range(max(first, 1), first + flock)):
-            post(fval_out.at[j], fval_in.at[mirror[j]], (row, who[j]), FINE, TO_FINE)
-        if first + flock == C:
-            tell(True)
+        lax.fori_loop(0, flock, fetch_turn, 0)
+        if behind is not None:
+            for j in reversed(range(max(behind, 1), behind + flock)):
+                post(fval_out.at[j], fval_in.at[mirror[j]], (row, who[j]), FINE, TO_FINE)
+            if turn_of <= 3:
+                tell(*((3, 3), (2, 2), (0, 1))[turn_of - 1])
     fval_in[0] = fval_out[0]
 
     place = lax.broadcasted_iota(jnp.int32, (BR, BC), 1)
@@ -717,7 +723,8 @@
             pltpu.VMEM((ITERS * ext, LANES), F32),
             pltpu.VMEM((blocks * TR, LANES), F32),
             pltpu.VMEM((ITERS * blocks * TR, LANES), F32),
-            pltpu.VMEM((ITERS * S, LANES), F32),
+            pltpu.VMEM((ITERS * S // 4, LANES), F32), pltpu.VMEM((ITERS * S // 4, LANES), F32),
+            pltpu.VMEM((C, 1, per), jnp.int32),
             pltpu.VMEM(((ITERS - 1) * TR, LANES), F32),
             pltpu.VMEM(((blocks + 1) * 48, LANES), F32),
             pltpu.VMEM((ITERS * (blocks + 1) * 48, LANES), F32),

time: 38.4 us -> 38.2 us (level)
  no operation moved by 1% of the time
where the time goes in v9:
time: 38.2 us; the launch traced here: 38 us
  Pallas kernels  37.4 us (98%)
  between operations  0.64 us (2%)
    pallas_call x1, Pallas kernels, per_device(): pl.pallas_call(functools.partial(kernel, R, C), out_shape=(pltpu.VMEM((TR...  36.4 us
    pallas_call x1, Pallas kernels, per_device(): pl.pallas_call(hand_over, out_shape=(jax.ShapeDtypeStruct((TR, TC), F32),...  1.02 us

profile of v9, /device:TPU:0, one launch (start us, length us, event | category | flops | bytes accessed | tf_op | source)
XLA Modules:
  0.0 38.0 jit_solution(12787392718382206239)
XLA Ops:
  0.6 36.4 %shard_map.95 = (f32[512,512]{1,0:T(8,128)S(1)}, f32[128,128]{1,0:T(8,128)S(1)}) custom-call(f32[512,512]{1,0:T(8,128)} %amp_in.1, s32[512,512]{1,0:T(8,128)} %mask_in.1, f32[512,512]{1,0:T(8,128)} %leak_in.1, f32[128,128]{1,0:T(8,128)} %cleak_in.1, f32[128,128]{1,0:T(8,128)} %cinit_in.1, s32[1,2048]{1,0:T(1,128)} %vf_in.1, s32[1,2048]{1,0:T(1,128)} %vc_in.1, ...), custom_call_target="tpu_custom_call" | custom-call | tf_op jit(solution)/shard_map/pallas_call | solution.py:705
  37.0 1.0 %shard_map.96 = (f32[512,512]{1,0:T(8,128)}, f32[128,128]{1,0:T(8,128)}) custom-call(f32[512,512]{1,0:T(8,128)S(1)} %get-tuple-element.4.x_in, f32[128,128]{1,0:T(8,128)S(1)} %get-tuple-element.5.c_in), custom_call_target="tpu_custom_call" | custom-call | tf_op jit(solution)/shard_map/pallas_call | solution.py:746

commit v10 on v9

--- a/solution.py
+++ b/solution.py
@@ -600,8 +600,8 @@
 
     for k in range(1, ITERS):
         for b, mask_of in edges:
-            held = side_v[pl.ds((k - 1) * TR, TR), :]
-            pltpu.store(V.at[ext(k, b, 16, TR), :], held, mask=mask_of)
+            at = ext(k, b, 16, TR)
+            V[at, :] = jnp.where(mask_of, side_v[pl.ds((k - 1) * TR, TR), :], V[at, :])
 
     arrive(cland.at[0], TO_COARSE)
     volt = cinit[...]

time: 38.2 us -> 38.2 us (level)
  no operation moved by 1% of the time
where the time goes in v10:
time: 38.2 us; the launch traced here: 38 us
  Pallas kernels  37.4 us (98%)
  between operations  0.64 us (2%)
    pallas_call x1, Pallas kernels, per_device(): pl.pallas_call(functools.partial(kernel, R, C), out_shape=(pltpu.VMEM((TR...  36.4 us
    pallas_call x1, Pallas kernels, per_device(): pl.pallas_call(hand_over, out_shape=(jax.ShapeDtypeStruct((TR, TC), F32),...  1.02 us

profile of v10, /device:TPU:0, one launch (start us, length us, event | category | flops | bytes accessed | tf_op | source)
XLA Modules:
  0.0 38.0 jit_solution(18158727851962441710)
XLA Ops:
  0.6 36.4 %shard_map.95 = (f32[512,512]{1,0:T(8,128)S(1)}, f32[128,128]{1,0:T(8,128)S(1)}) custom-call(f32[512,512]{1,0:T(8,128)} %amp_in.1, s32[512,512]{1,0:T(8,128)} %mask_in.1, f32[512,512]{1,0:T(8,128)} %leak_in.1, f32[128,128]{1,0:T(8,128)} %cleak_in.1, f32[128,128]{1,0:T(8,128)} %cinit_in.1, s32[1,2048]{1,0:T(1,128)} %vf_in.1, s32[1,2048]{1,0:T(1,128)} %vc_in.1, ...), custom_call_target="tpu_custom_call" | custom-call | tf_op jit(solution)/shard_map/pallas_call | solution.py:705
  37.0 1.0 %shard_map.96 = (f32[512,512]{1,0:T(8,128)}, f32[128,128]{1,0:T(8,128)}) custom-call(f32[512,512]{1,0:T(8,128)S(1)} %get-tuple-element.4.x_in, f32[128,128]{1,0:T(8,128)S(1)} %get-tuple-element.5.c_in), custom_call_target="tpu_custom_call" | custom-call | tf_op jit(solution)/shard_map/pallas_call | solution.py:746

commit v11 on v10

--- a/solution.py
+++ b/solution.py
@@ -63,7 +63,7 @@
     return side, tall, offsets, mirror, cuts, group
 
 
-MSG, VAL, FINE, RED, HALO, COARSE = 0, 1, 2, 3, 5, 7
+MSG, VAL, FINE, RED, HALO, COARSE = 0, 1, 2, 3, 4, 6
 PARTS = 4
 TO_MSG, TO_VAL, TO_FINE, TO_RED, TO_HALO, TO_COARSE, TO_CORNER = 0, 4, 8, 9, 10, 12, 14
 
@@ -178,7 +178,7 @@
     place_v[...] = (divide(fine_col, LANES) * TR + fine_row) * ITERS
     for j in range(C):
         lane_of[j] = remainder(fine_col, LANES)[:, j * per : (j + 1) * per]
-    move = pltpu.make_async_copy(place_v, place_s, load_sem.at[8])
+    move = pltpu.make_async_copy(place_v, place_s, load_sem.at[0])
     move.start()
     lanes = lax.broadcasted_iota(jnp.int32, (per, TC), 1).astype(F32)
     for j in range(C):
@@ -579,11 +579,16 @@
     place_u = lax.broadcasted_iota(jnp.int32, (BR, BC), 0)
     within = remainder(place, GROUP)
 
-    def beside(volt, n):
-        above = jnp.where(place_u == 0, keep(top_ok, cland[n, 15:16, :]), pltpu.roll(volt, 1, 0))
-        below = jnp.where(
-            place_u == BR - 1, keep(bot_ok, cland[n, 0:1, :]), pltpu.roll(volt, BR - 1, 0)
-        )
+    def within_block(volt):
+        above = jnp.where(place_u == 0, 0.0, pltpu.roll(volt, 1, 0))
+        below = jnp.where(place_u == BR - 1, 0.0, pltpu.roll(volt, BR - 1, 0))
+        before = jnp.where(within == 0, 0.0, pltpu.roll(volt, 1, 1))
+        after = jnp.where(within == GROUP - 1, 0.0, pltpu.roll(volt, BC - 1, 1))
+        return above + below + before + after
+
+    def from_others(n):
+        above = jnp.where(place_u == 0, keep(top_ok, cland[n, 15:16, :]), 0.0)
+        below = jnp.where(place_u == BR - 1, keep(bot_ok, cland[n, 0:1, :]), 0.0)
         group_at = lax.broadcasted_iota(jnp.int32, (groups, BR), 0)
         far = cland[n, 24:32, :]
         turn[n, pl.ds(0, groups, stride=GROUP), :] = jnp.where(
@@ -594,9 +599,8 @@
             right_ok, far, jnp.where(group_at == groups - 1, 0.0, jnp.roll(far, -1, 0))
         )
         edge = turn[n].T
-        before = jnp.where(within == 0, edge, pltpu.roll(volt, 1, 1))
-        after = jnp.where(within == GROUP - 1, edge, pltpu.roll(volt, BC - 1, 1))
-        return above + below + before + after
+        sides = jnp.where((within == 0) | (within == GROUP - 1), edge, 0.0)
+        return above + below + sides
 
     for k in range(1, ITERS):
         for b, mask_of in edges:
@@ -606,7 +610,7 @@
     arrive(cland.at[0], TO_COARSE)
     volt = cinit[...]
     scale = relaxation / coarse_diag
-    partial = volt + scale * (coarse_conductance * beside(volt, 0) - coarse_diag * volt)
+    partial = volt + scale * (coarse_conductance * (within_block(volt) + from_others(0)) - coarse_diag * volt)
     partial_turned, scale_turned = partial.T, scale.T
 
     arrive(red_in.at[pl.ds(1, R * C - 1)], TO_RED)
@@ -657,7 +661,9 @@
     volt = partial + scale * sources
     volt1[...] = volt
     coarse_send(volt1, 1)
-    partial = volt + scale * (sources - coarse_diag * volt)
+    partial = volt + scale * (
+        sources + coarse_conductance * within_block(volt) - coarse_diag * volt
+    )
     step = 64
 
     def finish(i, carry):
@@ -678,7 +684,7 @@
         drain(land.at[n], HALO + n)
         drain(cland.at[n], COARSE + n)
     arrive(cland.at[1], TO_COARSE + 1)
-    c_out[...] = partial + scale * (coarse_conductance * beside(volt, 1))
+    c_out[...] = partial + scale * (coarse_conductance * from_others(1))
 
 
 def hand_over(x_in, c_in, x_out, c_out, sem):
@@ -711,7 +717,7 @@
             pltpu.VMEM((TR, TC), F32), pltpu.VMEM((TR, TC), jnp.int32), pltpu.VMEM((TR, TC), F32),
             pltpu.VMEM((BR, BC), F32), pltpu.VMEM((BR, BC), F32),
             pltpu.VMEM((1, S), jnp.int32), pltpu.VMEM((1, S), jnp.int32),
-            pltpu.SMEM((1, C), jnp.int32), pltpu.SemaphoreType.DMA((9,)),
+            pltpu.SMEM((1, C), jnp.int32), pltpu.SemaphoreType.DMA((8,)),
             pltpu.VMEM((C, 1, per), jnp.int32), pltpu.VMEM((C, 1, per), jnp.int32),
             pltpu.VMEM((C, 1, per), F32), pltpu.VMEM((C, 1, per), F32),
             pltpu.VMEM((C, ITERS, per), F32), pltpu.VMEM((C, ITERS, per), F32),
@@ -735,7 +741,7 @@
             pltpu.VMEM((BR, BC), F32),
             pltpu.VMEM((2, BC, BR), F32), pltpu.VMEM((2, 2, BC // GROUP, BR), F32),
             pltpu.VMEM((2, 32, BC), F32),
-            pltpu.SemaphoreType.DMA((9,)),
+            pltpu.SemaphoreType.DMA((8,)),
             pltpu.SemaphoreType.DMA((16,)),
             pltpu.SemaphoreType.REGULAR,
         ],

time: 38.2 us -> 38.1 us (level)
  no operation moved by 1% of the time
where the time goes in v11:
time: 38.1 us; the launch traced here: 38 us
  Pallas kernels  37.4 us (98%)
  between operations  0.64 us (2%)
    pallas_call x1, Pallas kernels, per_device(): pl.pallas_call(functools.partial(kernel, R, C), out_shape=(pltpu.VMEM((TR...  36.3 us
    pallas_call x1, Pallas kernels, per_device(): pl.pallas_call(hand_over, out_shape=(jax.ShapeDtypeStruct((TR, TC), F32),...  1.02 us

profile of v11, /device:TPU:0, one launch (start us, length us, event | category | flops | bytes accessed | tf_op | source)
XLA Modules:
  0.0 38.0 jit_solution(1828132705481318217)
XLA Ops:
  0.6 36.3 %shard_map.95 = (f32[512,512]{1,0:T(8,128)S(1)}, f32[128,128]{1,0:T(8,128)S(1)}) custom-call(f32[512,512]{1,0:T(8,128)} %amp_in.1, s32[512,512]{1,0:T(8,128)} %mask_in.1, f32[512,512]{1,0:T(8,128)} %leak_in.1, f32[128,128]{1,0:T(8,128)} %cleak_in.1, f32[128,128]{1,0:T(8,128)} %cinit_in.1, s32[1,2048]{1,0:T(1,128)} %vf_in.1, s32[1,2048]{1,0:T(1,128)} %vc_in.1, ...), custom_call_target="tpu_custom_call" | custom-call | tf_op jit(solution)/shard_map/pallas_call | solution.py:711
  37.0 1.0 %shard_map.96 = (f32[512,512]{1,0:T(8,128)}, f32[128,128]{1,0:T(8,128)}) custom-call(f32[512,512]{1,0:T(8,128)S(1)} %get-tuple-element.4.x_in, f32[128,128]{1,0:T(8,128)S(1)} %get-tuple-element.5.c_in), custom_call_target="tpu_custom_call" | custom-call | tf_op jit(solution)/shard_map/pallas_call | solution.py:752
